TPU v7x, 32 devices: a whole 2x2x4 slice. The times are simulated.
32 devices in a mesh: groups: 2 (over x), seq: 8 (over z, y), dec: 2 (over core).
Axes of the slice: x: 2, y: 2, z: 4, core: 2. Of those that a mesh axis runs over, the one named last changes fastest.
Arguments:
- tokens: bfloat16 [2048, 4096], P(('groups', 'seq')), parts along dimension 0, may hold values from -64 to 64
- norm_gain: float32 [4096], replicated, may hold values from 0.25 to 1.75
- w_query: bfloat16 [4096, 2048], P('seq', 'dec'), may hold values from -0.140625 to 0.140625
- w_key: bfloat16 [4096, 512], P('seq', 'dec'), may hold values from -0.140625 to 0.140625
- w_value: bfloat16 [4096, 512], P('seq', 'dec'), may hold values from -0.09375 to 0.09375
- block_order: int32 [32], P('groups'), parts along dimension 0, may hold values from 0 to 15, as said below
- block_docs: int32 [32], P('groups'), parts along dimension 0, may hold values from 0 to 3, never falling along the last dimension, each value on 1 to 8 neighbouring positions
- head_owner: int32 [8], P('groups'), parts along dimension 0, may hold values from 0 to 3, as said below
- prev_kv: bfloat16 [2048, 2, 4, 128], P(('groups', 'seq', 'dec')), parts along dimension 0, may hold values from -6 to 6
Outputs:
- attended: bfloat16 [2048, 2048], P(('groups', 'seq'), 'dec'), parts along dimension 0
- decode_cache: bfloat16 [2048, 2, 4, 128], P(('groups', 'seq'), None, 'dec'), parts along dimension 0
There are 2 independent parts, one for each index of `groups`. A program takes and returns all parts, laid end to end along the dimension named above; an argument that names none is the same for every part. Nothing has to cross between parts.
Inputs may be any that keep to these rules, and one draw needn't show every extreme that they name: `block_order`: cycle slots 2i and 2i + 1 hold the blocks b and 15 - b for some b; every block stands in exactly one slot. `head_owner`: each key-value head stands in exactly one decode slot.
All inputs are finite; a program needn't handle non-finite values.
Results may differ from a plain program's by a relative error of at most 0.0035.
The roundings to bfloat16 on the way count: a program that leaves them out, or rounds other values in their place, can miss the bound.
Values may be sent and summed in bfloat16 or wider, within the bound.
A program may use at most 64 MiB of HBM per device.

v0:
```python
import functools
import math

import jax
import jax.numpy as jnp
from jax import lax
from jax.experimental import pallas as pl
from jax.experimental.pallas import tpu as pltpu
from jax.sharding import PartitionSpec as P

HD = 128


def rotate(values, positions):
    half_width = values.shape[-1] // 2
    frequency = 500000.0 ** (-jnp.arange(half_width, dtype=jnp.float32) / half_width)
    angles = positions[:, None].astype(jnp.float32) * frequency[None, :]
    cosines = jnp.cos(angles)[:, None, :]
    sine_terms = jnp.sin(angles)[:, None, :]
    lower_half = values[..., :half_width]
    upper_half = values[..., half_width:]
    return jnp.concatenate(
        [
            lower_half * cosines - upper_half * sine_terms,
            upper_half * cosines + lower_half * sine_terms,
        ],
        -1,
    )


def general_plan(
    tokens, norm_gain, w_query, w_key, w_value, block_order, block_docs, head_owner, prev_kv
):
    rows_dev = tokens.shape[0]
    block_rows = rows_dev // 2
    inputs = tokens.astype(jnp.float32)
    normed = (
        inputs * lax.rsqrt(jnp.mean(inputs * inputs, -1, keepdims=True) + 1e-05) * norm_gain
    ).astype(jnp.bfloat16)

    def add_piece(piece):
        return jnp.dot(normed, piece, preferred_element_type=jnp.float32)

    pieces = (
        lax.all_gather(w_query, "seq", axis=0, tiled=True),
        lax.all_gather(w_key, "seq", axis=0, tiled=True),
        lax.all_gather(w_value, "seq", axis=0, tiled=True),
    )
    query_full, key_full, value_full = tuple((add_piece(piece) for piece in pieces))
    total_rows = rows_dev * lax.axis_size("seq")
    row_ids = jnp.arange(total_rows, dtype=jnp.int32)
    natural = jnp.take(block_order, row_ids // block_rows)
    pos_all = natural * block_rows + row_ids % block_rows
    doc_all = jnp.take(block_docs, natural)
    offset = lax.axis_index("seq") * rows_dev
    my_pos = lax.dynamic_slice_in_dim(pos_all, offset, rows_dev)
    my_doc = lax.dynamic_slice_in_dim(doc_all, offset, rows_dev)
    local_kv = key_full.shape[1] // HD
    local_heads = query_full.shape[1] // HD
    group_size = local_heads // local_kv
    queries = rotate(query_full.reshape(rows_dev, local_heads, HD), my_pos).astype(jnp.bfloat16)
    query_groups = queries.reshape(rows_dev, local_kv, group_size, HD).transpose(1, 2, 0, 3)
    key_rows = (
        rotate(key_full.reshape(rows_dev, local_kv, HD), my_pos)
        .astype(jnp.bfloat16)
        .reshape(rows_dev, local_kv * HD)
    )
    value_rows = value_full.astype(jnp.bfloat16)
    scale = 1.0 / math.sqrt(HD)
    start_max = jnp.full((local_kv, group_size, rows_dev, 1), -jnp.inf, jnp.float32)
    start_sum = jnp.zeros((local_kv, group_size, rows_dev, 1), jnp.float32)
    start_weighted = jnp.zeros((local_kv, group_size, rows_dev, HD), jnp.float32)
    key_piece = lax.all_gather(key_rows, "seq", axis=0, tiled=True)
    value_piece = lax.all_gather(value_rows, "seq", axis=0, tiled=True)
    count = key_piece.shape[0]
    allowed = (pos_all[None, :] <= my_pos[:, None]) & (doc_all[None, :] == my_doc[:, None])

    def update(state):
        running_max, running_sum, weighted = state
        scores = (
            jnp.einsum(
                "ghtd,sgd->ghts",
                query_groups,
                key_piece.reshape(count, local_kv, HD),
                preferred_element_type=jnp.float32,
            )
            * scale
        )
        scores = jnp.where(allowed, scores, -jnp.inf)
        new_max = jnp.max(scores, -1, keepdims=True)
        shift_by = jnp.where(new_max == -jnp.inf, 0.0, new_max)
        weights = jnp.exp(scores - shift_by)
        rescale = jnp.exp(running_max - shift_by)
        running_sum = running_sum * rescale + jnp.sum(weights, -1, keepdims=True)
        weighted = weighted * rescale + jnp.einsum(
            "ghts,sgd->ghtd",
            weights.astype(jnp.bfloat16),
            value_piece.reshape(count, local_kv, HD),
            preferred_element_type=jnp.float32,
        )
        return (new_max, running_sum, weighted)

    final_max, final_sum, final_weighted = lax.cond(
        jnp.any(allowed), update, lambda state: state, (start_max, start_sum, start_weighted)
    )
    attended = (
        (final_weighted / final_sum)
        .transpose(2, 0, 1, 3)
        .reshape(rows_dev, local_heads * HD)
        .astype(jnp.bfloat16)
    )
    head_count = prev_kv.shape[2]
    selector = (head_owner[:, None] == jnp.arange(head_count, dtype=jnp.int32)[None, :]).astype(
        jnp.bfloat16
    )
    ordered = jnp.einsum(
        "tcjd,sj->tcsd", prev_kv, selector, preferred_element_type=jnp.float32
    ).astype(jnp.bfloat16)
    decode_cache = lax.all_to_all(ordered, "dec", split_axis=2, concat_axis=0, tiled=True)
    return (attended, decode_cache)


def attend_kernel(
    sizes,
    order_ref,
    docs_ref,
    freq_ref,
    gain_ref,
    tok_in,
    wq_in,
    wk_in,
    wv_in,
    prev_in,
    out_ref,
    prev_out,
    tok,
    wbuf,
    normed,
    qbuf,
    kvbuf,
    csbuf,
    att,
    local_sem,
    home_send,
    homeq_recv,
    homekv_recv,
    rel_send,
    rel_recv,
    own_send,
    fwd_send,
    tok_recv,
    sib_send,
    sib_recv,
    prev_sem,
    kv_send,
    kv_recv,
    att_send,
    att_recv,
):
    X, A, Y, rows, R, hpg, slots, blk, T = sizes
    Rp = R // X
    half = rows // 2
    QW = hpg * HD
    x = lax.axis_index("groups")
    q = lax.axis_index("seq")
    d = lax.axis_index("dec")
    a = q // Y
    y = q % Y
    unit = a % 2

    def dev(x_, a_, y_, d_=None):
        return {"groups": x_, "seq": a_ * Y + y_, "dec": d if d_ is None else d_}

    def remote(src, dst, ssem, rsem, device):
        return pltpu.make_async_remote_copy(
            src_ref=src,
            dst_ref=dst,
            send_sem=ssem,
            recv_sem=rsem,
            device_id=device,
            device_id_type=pl.DeviceIdType.MESH,
        )

    sibling = dev(x, a, y, 1 - d)
    barrier = pltpu.get_barrier_semaphore()
    plane = [(i, j) for i in range(X) for j in range(Y) if (i, j) != (0, 0)]
    peers = [dev((x + i) % X, a, (y + j) % Y) for i, j in plane]
    peers += [dev(x, (a + t) % A, y) for t in range(1, A)]
    mate = a + 1 - 2 * unit
    peers += [dev(x, mate, (y + j) % Y) for j in range(1, Y)]
    peers.append(sibling)
    for peer in peers:
        pl.semaphore_signal(barrier, inc=1, device_id=peer, device_id_type=pl.DeviceIdType.MESH)
    pl.semaphore_wait(barrier, len(peers))

    def w_rows(a_, y_, x_):
        return pl.ds(pl.multiple_of((a_ * Y + y_) * R + x_ * Rp, Rp), Rp)

    part = pl.ds(pl.multiple_of(x * Rp, Rp), Rp)

    def kv_source(t):
        return wv_in if t % 2 else wk_in

    def home_copies(t):
        kv_cols = pl.ds((t // 2) * HD, HD)
        return (
            remote(
                wq_in.at[part, pl.ds(t * QW, QW)],
                wbuf.at[w_rows(a, y, x), pl.ds(0, QW)],
                home_send.at[0, t],
                homeq_recv.at[a],
                dev(x, t, y),
            ),
            remote(
                kv_source(t).at[part, kv_cols],
                wbuf.at[w_rows(a, y, x), pl.ds(QW, HD)],
                home_send.at[1, t],
                homekv_recv.at[a],
                dev(x, t, y),
            ),
        )

    def local_copies(t):
        rows_all = pl.ds(pl.multiple_of(q * R, R), R)
        return (
            pltpu.make_async_copy(
                wq_in.at[:, pl.ds(t * QW, QW)],
                wbuf.at[rows_all, pl.ds(0, QW)],
                local_sem.at[0],
            ),
            pltpu.make_async_copy(
                kv_source(t).at[:, pl.ds((t // 2) * HD, HD)],
                wbuf.at[rows_all, pl.ds(QW, HD)],
                local_sem.at[1],
            ),
        )

    for t in range(A):

        @pl.when(a == t)
        def _():
            for copy in local_copies(t):
                copy.start()

        @pl.when(a != t)
        def _():
            for copy in home_copies(t):
                copy.start()

    my_half = pl.ds(pl.multiple_of(d * half, half), half)
    other_half = pl.ds(pl.multiple_of((1 - d) * half, half), half)

    def own_push(side):
        return remote(
            tok_in.at[my_half],
            tok.at[a, my_half],
            own_send.at[side],
            tok_recv.at[a],
            dev(x, a + 1 - 2 * side, y),
        )

    @pl.when(a + 1 < A)
    def _():
        own_push(0).start()

    @pl.when(a >= 1)
    def _():
        own_push(1).start()

    own_tok = pltpu.make_async_copy(tok_in, tok.at[a], local_sem.at[2])
    own_tok.start()
    prev_copy = remote(prev_in, prev_out, prev_sem.at[0], prev_sem.at[1], sibling)
    prev_copy.start()

    def relay(t, index, i, j):
        src = wbuf.at[w_rows(t, y, x)]
        return remote(
            src,
            src,
            rel_send.at[t, index],
            rel_recv.at[t, y, x],
            dev((x + i) % X, a, (y + j) % Y),
        )

    for t in range(A):

        @pl.when(a == t)
        def _():
            for copy in local_copies(t):
                copy.wait()
            for index, (i, j) in enumerate(plane):
                if j:
                    relay(t, index, i, j).start()

    lane = lax.broadcasted_iota(jnp.int32, (rows, HD), 1)
    row_id = lax.broadcasted_iota(jnp.int32, (rows, 1), 0)

    def row_values(c, table):
        value = jnp.zeros((rows, 1), jnp.int32)
        for i in range(slots):
            entry = table(order_ref[(c * Y + y) * slots + i])
            value = jnp.where(row_id // blk == i, entry, value)
        return value

    def row_positions(c):
        return row_values(c, lambda n: n) * blk + row_id % blk

    for o in range(1, A):
        t = (a + o) % A
        src = wbuf.at[w_rows(t, y, x)]
        remote(
            wq_in.at[part, pl.ds(0, QW)],
            wbuf.at[w_rows(t, y, x), pl.ds(0, QW)],
            home_send.at[0, 0],
            homeq_recv.at[t],
            sibling,
        ).wait_recv()
        remote(
            wk_in.at[part, pl.ds(0, HD)],
            wbuf.at[w_rows(t, y, x), pl.ds(QW, HD)],
            home_send.at[1, 0],
            homekv_recv.at[t],
            sibling,
        ).wait_recv()
        for index, (i, j) in enumerate(plane):
            relay(t, index, i, j).start()

    def forward(c, to):
        return remote(
            tok.at[c, my_half],
            tok.at[c, my_half],
            fwd_send.at[c],
            tok_recv.at[c],
            dev(x, to, y),
        )

    def share(c):
        return remote(
            tok.at[c, my_half], tok.at[c, my_half], sib_send.at[c], sib_recv.at[c], sibling
        )

    def token_step(s):
        @pl.when(a >= s)
        def _():
            c = a - s
            forward(c, a).wait_recv()

            @pl.when(a + 1 < A)
            def _():
                forward(c, a + 1).start()

            share(c).start()

        @pl.when(a + s < A)
        def _():
            c = a + s
            forward(c, a).wait_recv()

            @pl.when(a >= 1)
            def _():
                forward(c, a - 1).start()

            share(c).start()

    def pick(s):
        value, bit = 0, 1
        while bit < A:
            value = value + bit * ((a // bit + s // bit) % 2)
            bit *= 2
        return value

    def kv_peer(dy, da):
        return dev(x, a - unit + (unit + da) % 2, (y + dy) % Y)

    kv_plan = [(dy, da) for dy in range(Y) for da in range(2) if (dy, da) != (0, 0)]

    def kv_push(s, c, index, dy, da):
        src = kvbuf.at[unit, c * Y + y]
        return remote(src, src, kv_send.at[s, index], kv_recv.at[unit, c, y], kv_peer(dy, da))

    def normalize(s):
        c = pick(s)
        if s == 0:
            own_tok.wait()
        else:
            other = tok.at[c, other_half]
            remote(other, other, sib_send.at[c], sib_recv.at[c], sibling).wait_recv()

        def block(i, carry):
            span = pl.ds(pl.multiple_of(i * 16, 16), 16)
            inputs = tok[c, span].astype(jnp.float32)
            mean = jnp.mean(inputs * inputs, -1, keepdims=True)
            normed[c, span] = (inputs * lax.rsqrt(mean + 1e-05) * gain_ref[...]).astype(
                jnp.bfloat16
            )
            return carry

        lax.fori_loop(0, rows // 16, block, 0, unroll=2)

    def project(s, carry):
        c = pick(s)
        cosine = csbuf[0, c]
        sine = csbuf[1, c]

        def turn(v):
            return v * cosine + pltpu.roll(v, HD // 2, 1) * sine

        raw = jnp.dot(normed[c], wbuf[:, QW:], preferred_element_type=jnp.float32)
        kvbuf[unit, c * Y + y] = jnp.where(unit == 0, turn(raw), raw).astype(jnp.bfloat16)
        product = jnp.dot(normed[c], wbuf[:, :QW], preferred_element_type=jnp.float32)
        for index, (dy, da) in enumerate(kv_plan):
            kv_push(s, c, index, dy, da).start()
        for h in range(hpg):
            qbuf[c, :, h * HD : (h + 1) * HD] = turn(product[:, h * HD : (h + 1) * HD]).astype(
                jnp.bfloat16
            )
        return carry

    step_angle = (row_id % blk).astype(jnp.float32) * freq_ref[...]
    step_cos = jnp.cos(step_angle)
    step_sin = jnp.sin(step_angle)
    sign = jnp.where(lane < HD // 2, -1.0, 1.0)
    entry_id = lax.broadcasted_iota(jnp.int32, (A * slots, 1), 0)
    entries = jnp.zeros((A * slots, 1), jnp.int32)
    for c in range(A):
        for i in range(slots):
            entries = jnp.where(
                entry_id == c * slots + i, order_ref[(c * Y + y) * slots + i], entries
            )
    base_angle = (entries * blk).astype(jnp.float32) * freq_ref[...]
    base_cos = jnp.cos(base_angle)
    base_sin = jnp.sin(base_angle)
    for c in range(A):
        row_cos = jnp.broadcast_to(base_cos[c * slots : c * slots + 1], (rows, HD))
        row_sin = jnp.broadcast_to(base_sin[c * slots : c * slots + 1], (rows, HD))
        for i in range(1, slots):
            k = c * slots + i
            row_cos = jnp.where(row_id // blk == i, base_cos[k : k + 1], row_cos)
            row_sin = jnp.where(row_id // blk == i, base_sin[k : k + 1], row_sin)
        csbuf[0, c] = row_cos * step_cos - row_sin * step_sin
        csbuf[1, c] = (row_sin * step_cos + row_cos * step_sin) * sign

    normalize(0)
    for s in range(1, A - 1):
        token_step(s)
        normalize(s)
    for o in range(A):
        t = (a + o) % A
        for i, j in plane:
            if o or j:
                src = wbuf.at[w_rows(t, (y + j) % Y, (x + i) % X)]
                remote(
                    src,
                    src,
                    rel_send.at[0, 0],
                    rel_recv.at[t, (y + j) % Y, (x + i) % X],
                    sibling,
                ).wait_recv()

    lax.fori_loop(0, A - 1, project, 0)
    token_step(A - 1)
    normalize(A - 1)
    project(A - 1, 0)

    for s in range(A):
        c = pick(s)
        for dy, da in kv_plan:
            u = (unit + da) % 2
            dst = kvbuf.at[u, c * Y + (y + dy) % Y]
            remote(
                dst, dst, kv_send.at[0, 0], kv_recv.at[u, c, (y + dy) % Y], sibling
            ).wait_recv()

    key_id = lax.broadcasted_iota(jnp.int32, (1, T), 1)
    key_pos = jnp.zeros((1, T), jnp.int32)
    key_doc = jnp.zeros((1, T), jnp.int32)
    for i in range(T // blk):
        here = key_id // blk == i
        natural = order_ref[i]
        key_pos = jnp.where(here, natural * blk, key_pos)
        key_doc = jnp.where(here, docs_ref[natural], key_doc)
    key_pos = key_pos + key_id % blk
    scale = 1.0 / math.sqrt(HD)
    out_cols = pl.ds(pl.multiple_of(a * QW, QW), QW)

    def att_push(s, c):
        return remote(
            att.at[c], out_ref.at[:, out_cols], att_send.at[s], att_recv.at[a], dev(x, c, y)
        )

    def attend(s, carry):
        c = pick(A - 1 - s)
        allowed = (key_pos <= row_positions(c)) & (
            key_doc == row_values(c, lambda n: docs_ref[n])
        )
        keys = kvbuf[0].reshape(T, HD)
        values = kvbuf[1].reshape(T, HD)
        for h in range(hpg):
            scores = (
                lax.dot_general(
                    qbuf[c, :, h * HD : (h + 1) * HD],
                    keys,
                    (((1,), (1,)), ((), ())),
                    preferred_element_type=jnp.float32,
                )
                * scale
            )
            scores = jnp.where(allowed, scores, -jnp.inf)
            weights = jnp.exp(scores - jnp.max(scores, -1, keepdims=True))
            total = jnp.sum(weights, -1, keepdims=True)
            weighted = jnp.dot(
                weights.astype(jnp.bfloat16), values, preferred_element_type=jnp.float32
            )
            att[c, :, h * HD : (h + 1) * HD] = (weighted / total).astype(jnp.bfloat16)

        @pl.when(s < A - 1)
        def _():
            att_push(s, c).start()

        return carry

    lax.fori_loop(0, A, attend, 0)
    own_out = pltpu.make_async_copy(att.at[a], out_ref.at[:, out_cols], local_sem.at[3])
    own_out.start()

    for t in range(A):

        @pl.when(a != t)
        def _():
            for copy in home_copies(t):
                copy.wait_send()
            for index, (i, j) in enumerate(plane):
                relay(t, index, i, j).wait_send()

        @pl.when(a == t)
        def _():
            for index, (i, j) in enumerate(plane):
                if j:
                    relay(t, index, i, j).wait_send()

    @pl.when(a + 1 < A)
    def _():
        own_push(0).wait_send()

    @pl.when(a >= 1)
    def _():
        own_push(1).wait_send()

    for s in range(1, A):

        @pl.when(a >= s)
        def _():
            share(a - s).wait_send()

            @pl.when(a + 1 < A)
            def _():
                forward(a - s, a + 1).wait_send()

        @pl.when(a + s < A)
        def _():
            share(a + s).wait_send()

            @pl.when(a >= 1)
            def _():
                forward(a + s, a - 1).wait_send()

    for s in range(A):
        for index, (dy, da) in enumerate(kv_plan):
            kv_push(s, pick(s), index, dy, da).wait_send()
    prev_copy.wait()
    own_out.wait()
    for s in range(A - 1):
        att_push(s, pick(A - 1 - s)).wait_send()
    for o in range(1, A):
        t = (a + o) % A
        cols = pl.ds(pl.multiple_of(t * QW, QW), QW)
        remote(
            att.at[0], out_ref.at[:, cols], att_send.at[0], att_recv.at[t], sibling
        ).wait_recv()


def column_plan(
    X, tokens, norm_gain, w_query, w_key, w_value, block_order, block_docs, head_owner, prev_kv
):
    n_seq = lax.axis_size("seq")
    rows, width = tokens.shape
    R = w_query.shape[0]
    local_kv = w_key.shape[1] // HD
    local_heads = w_query.shape[1] // HD
    A = 2 * local_kv
    Y = n_seq // A
    hpg = local_heads // A
    slots = block_order.shape[0] // n_seq
    blk = rows // slots
    T = n_seq * rows
    QW = hpg * HD
    frequency = 500000.0 ** (-jnp.arange(HD // 2, dtype=jnp.float32) / (HD // 2))
    freq = jnp.concatenate([frequency, frequency])[None, :]
    sizes = (X, A, Y, rows, R, hpg, slots, blk, T)
    dma = pltpu.SemaphoreType.DMA
    smem = pl.BlockSpec(memory_space=pltpu.SMEM)
    vmem = pl.BlockSpec(memory_space=pltpu.VMEM)
    anywhere = pl.BlockSpec(memory_space=pl.ANY)
    attended, other = pl.pallas_call(
        functools.partial(attend_kernel, sizes),
        out_shape=(
            jax.ShapeDtypeStruct((rows, local_heads * HD), jnp.bfloat16),
            jax.ShapeDtypeStruct(prev_kv.shape, prev_kv.dtype),
        ),
        in_specs=[smem, smem, vmem, vmem] + [anywhere] * 5,
        out_specs=(vmem, anywhere),
        scratch_shapes=[
            pltpu.VMEM((A, rows, width), jnp.bfloat16),
            pltpu.VMEM((width, QW + HD), jnp.bfloat16),
            pltpu.VMEM((A, rows, width), jnp.bfloat16),
            pltpu.VMEM((A, rows, QW), jnp.bfloat16),
            pltpu.VMEM((2, n_seq, rows, HD), jnp.bfloat16),
            pltpu.VMEM((2, A, rows, HD), jnp.float32),
            pltpu.VMEM((A, rows, QW), jnp.bfloat16),
            dma((4,)),
            dma((2, A)),
            dma((A,)),
            dma((A,)),
            dma((A, X * Y)),
            dma((A, Y, X)),
            dma((2,)),
            dma((A,)),
            dma((A,)),
            dma((A,)),
            dma((A,)),
            dma((2,)),
            dma((A, 2 * Y)),
            dma((2, A, Y)),
            dma((A,)),
            dma((A,)),
        ],
        compiler_params=pltpu.CompilerParams(
            collective_id=0, has_side_effects=True
        ),
    )(
        block_order,
        block_docs,
        freq,
        norm_gain[None, :],
        tokens,
        w_query,
        w_key,
        w_value,
        prev_kv,
    )
    d = lax.axis_index("dec")
    head_count = prev_kv.shape[2]
    mine = head_count // 2
    owner = lax.dynamic_slice_in_dim(head_owner, d * mine, mine)
    both = jnp.concatenate(
        [jnp.where(d == 0, prev_kv, other), jnp.where(d == 0, other, prev_kv)], 0
    )
    picks = []
    for s in range(mine):
        chosen = both[:, :, 0]
        for j in range(1, head_count):
            chosen = jnp.where(owner[s] == j, both[:, :, j], chosen)
        picks.append(chosen)
    return attended, jnp.stack(picks, 2)


def solution(mesh):
    in_specs = (
        P(("groups", "seq"), None),
        P(),
        P("seq", "dec"),
        P("seq", "dec"),
        P("seq", "dec"),
        P("groups"),
        P("groups"),
        P("groups"),
        P(("groups", "seq", "dec"), None, None, None),
    )
    out_specs = (P(("groups", "seq"), "dec"), P(("groups", "seq"), None, "dec", None))
    X = mesh.shape["groups"]
    n_seq = mesh.shape["seq"]

    def per_device(tokens, norm_gain, w_query, w_key, w_value, *rest):
        A = 2 * (w_key.shape[1] // HD)
        heads = w_query.shape[1] // HD
        fits = (
            mesh.shape["dec"] == 2
            and A & (A - 1) == 0
            and n_seq % A == 0
            and heads % A == 0
            and w_query.shape[0] % (16 * X) == 0
            and tokens.shape[0] % 32 == 0
        )
        plan = functools.partial(column_plan, X) if fits else general_plan
        return plan(tokens, norm_gain, w_query, w_key, w_value, *rest)

    return jax.shard_map(
        per_device, mesh=mesh, in_specs=in_specs, out_specs=out_specs, check_vma=False
    )
```

profile of v0, /device:TPU:0, one launch (start us, length us, event | category | flops | bytes accessed | tf_op | source)
XLA Modules:
  0.0 87.0 jit_solution(1806614724321296268)
XLA Ops:
  0.6 0.0 copy-start.2
  0.6 0.6 copy-done.2
  1.3 0.1 dynamic_slice.3
  1.4 0.6 maximum_bitcast_fusion.freq_ref
  2.0 0.7 fusion.3
  6.7 0.0 copy-start
  6.7 77.1 %shard_map.104 = (bf16[128,1024]{1,0:T(8,128)(2,1)}, bf16[64,2,4,128]{3,2,1,0:T(4,128)(2,1)}) custom-call(s32[16]{0:T(128)} %order_ref.1, s32[16]{0:T(128)} %docs_ref.1, f32[1,128]{1,0:T(1,128)} %maximum_bitcast_fusion.freq_ref, f32[1,4096]{1,0:T(1,128)} %bitcast.17, bf16[128,4096]{1,0:T(8,128)(2,1)} %tok_in.1, bf16[512,1024]{1,0:T(8,128)(2,1)} %wq_in.1, ...), custom_call_target="tpu_custom_call" | custom-call | tf_op jit(solution)/shard_map/pallas_call | solution.py:604
  83.8 0.0 copy-done
  83.8 0.9 %broadcast_select_fusion.7 = (bf16[64,1,8,128]{3,2,1,0:T(8,128)(2,1)S(1)}, bf16[64,1,8,128]{3,2,1,0:T(8,128)(2,1)S(1)}) fusion(bf16[64,1,8,128]{3,2,1,0:T(8,128)(2,1)S(1)} %bitcast.13, bf16[64,1,8,128]{3,2,1,0:T(8,128)(2,1)} %bitcast.16, pred[]{:T(512)S(6)} %eq.42), kind=kLoop, calls=%fused_computation.18 | loop fusion | flops 131072 | bytes 524289 | tf_op jit(solution)/shard_map/jit(_where)/select_n | solution.py:656
  84.7 0.5 broadcast_select_fusion.5
  85.3 0.0 copy-start.1
  85.3 1.0 %pad_maximum_fusion.1 = bf16[128,2,2,128]{3,2,1,0:T(2,128)(2,1)} fusion(bf16[128,2,1,128]{3,2,1,0:T(2,128)(2,1)S(1)} %get-tuple-element.7, bf16[128,2,1,128]{3,2,1,0:T(2,128)(2,1)S(1)} %get-tuple-element.6), kind=kLoop, calls=%fused_computation.16 | loop fusion | flops 262144 | bytes 262144 | tf_op jit(solution)/shard_map/stack | solution.py:664
  86.2 0.0 copy-done.1
  86.2 0.7 copy.12
  (1 shorter events, 0.0 us)
Async XLA Ops:
  0.6 0.7 copy-start.2
  6.7 77.1 %copy-start = (bf16[64,2,4,128]{3,2,1,0:T(4,128)(2,1)S(1)}, bf16[64,2,4,128]{3,2,1,0:T(4,128)(2,1)}, u32[]{:S(2)}) copy-start(bf16[64,2,4,128]{3,2,1,0:T(4,128)(2,1)} %prev_in.1) | copy-start | bytes 393220
  85.3 1.0 %copy-start.1 = (bf16[128,1024]{1,0:T(8,128)(2,1)S(1)}, bf16[128,1024]{1,0:T(8,128)(2,1)}, u32[]{:S(2)}) copy-start(bf16[128,1024]{1,0:T(8,128)(2,1)} %get-tuple-element.16) | copy-start | bytes 786436
where the time goes:
time: 87.2 us; the launch traced here: 87 us
  Pallas kernels  77.1 us (88%)
  between operations  4.71 us (5%)
  other arithmetic  3.04 us (3%)
  local copies, waits for them, and re-layouts  2.1 us (2%)
    pallas_call x1, Pallas kernels, column_plan(): pl.pallas_call(functools.partial(attend_kernel, sizes), out_shape=(jax.Sh...  77.1 us

commit v1 on v0

--- a/solution.py
+++ b/solution.py
@@ -3,6 +3,7 @@
 
 import jax
 import jax.numpy as jnp
+import numpy as np
 from jax import lax
 from jax.experimental import pallas as pl
 from jax.experimental.pallas import tpu as pltpu
@@ -664,6 +665,590 @@
     return attended, jnp.stack(picks, 2)
 
 
+def quad_kernel(
+    sizes,
+    order_ref,
+    docs_ref,
+    owner_ref,
+    freq_in,
+    gain_in,
+    tok_in,
+    wq_in,
+    wk_in,
+    wv_in,
+    prev_in,
+    out_ref,
+    cache_ref,
+    freq,
+    gain,
+    tokraw,
+    wbuf,
+    normed,
+    qbuf,
+    acc,
+    kvbuf,
+    csbuf,
+    bias,
+    att,
+    prev,
+    picked,
+    local_sem,
+    init_send,
+    far_send,
+    pair_send,
+    w_recv,
+    own_send,
+    pass_send,
+    share_send,
+    tok_recv,
+    sib_recv,
+    kv_send,
+    kv_recv,
+    att_send,
+    att_recv,
+    out_sem,
+    cache_sem,
+):
+    A, rows, R, hpg, slots, blk, T, chunks, heads = sizes
+    Rp = R // 2
+    half = rows // 2
+    step = half // chunks
+    x = lax.axis_index("groups")
+    q = lax.axis_index("seq")
+    d = lax.axis_index("dec")
+    g = q // A
+    c = q % A
+    u = c // 2
+    y = c % 2
+
+    def near(du, dy):
+        return ((u + du) % 2) * 2 + (y + dy) % 2
+
+    across_y, across_z, across = near(0, 1), near(1, 0), near(1, 1)
+
+    def dev(x_, q_, d_):
+        return {"groups": x_, "seq": q_, "dec": d_}
+
+    def remote(src, dst, ssem, rsem, device):
+        return pltpu.make_async_remote_copy(
+            src_ref=src,
+            dst_ref=dst,
+            send_sem=ssem,
+            recv_sem=rsem,
+            device_id=device,
+            device_id_type=pl.DeviceIdType.MESH,
+        )
+
+    sibling = dev(x, q, 1 - d)
+    pair = dev(1 - x, q, d)
+    far = dev(x, (1 - g) * A + c, d)
+    quad = [dev(x, g * A + t, d) for t in (across_y, across_z, across)]
+
+    def w_at(piece, source, part):
+        return wbuf.at[piece, pl.ds(pl.multiple_of(source * R + part * Rp, Rp), Rp)]
+
+    part_rows = pl.ds(pl.multiple_of(x * Rp, Rp), Rp)
+
+    def start_weights(piece, t, dst, ssem, rsem, device, span):
+        def go(source, column):
+            src = source.at[span, pl.ds(pl.multiple_of(column, HD), HD)]
+            if device is None:
+                pltpu.make_async_copy(src, dst, ssem).start()
+            else:
+                remote(src, dst, ssem, rsem, device).start()
+
+        if piece:
+            go(wq_in, (t * hpg + piece - 1) * HD)
+        else:
+
+            @pl.when(t % 2 == 0)
+            def _():
+                go(wk_in, (t // 2) * HD)
+
+            @pl.when(t % 2 == 1)
+            def _():
+                go(wv_in, (t // 2) * HD)
+
+    pieces = hpg + 1
+    my_half = pl.ds(pl.multiple_of(d * half, half), half)
+    tok_copy = pltpu.make_async_copy(tok_in.at[my_half], tokraw, local_sem.at[pieces])
+    tok_copy.start()
+    gain_copy = pltpu.make_async_copy(gain_in, gain, local_sem.at[pieces + 1])
+    gain_copy.start()
+    freq_copy = pltpu.make_async_copy(freq_in, freq, local_sem.at[pieces + 2])
+    freq_copy.start()
+    prev_copy = pltpu.make_async_copy(prev_in, prev, local_sem.at[pieces + 3])
+    prev_copy.start()
+
+    def own_rows(piece):
+        return wbuf.at[piece, pl.ds(pl.multiple_of(q * R, R), R)]
+
+    for piece in range(pieces):
+        start_weights(
+            piece, c, own_rows(piece), local_sem.at[piece], None, None, pl.ds(0, R)
+        )
+
+    barrier = pltpu.get_barrier_semaphore()
+    peers = quad + [far, pair, sibling]
+    for peer in peers:
+        pl.semaphore_signal(barrier, inc=1, device_id=peer, device_id_type=pl.DeviceIdType.MESH)
+    pl.semaphore_wait(barrier, len(peers))
+
+    def first_sends(piece):
+        targets = [(c, far), (across, quad[2]), (across_z, quad[1]), (across_y, quad[0])]
+        for i, (t, device) in enumerate(targets):
+            start_weights(
+                piece,
+                t,
+                w_at(piece, q, x),
+                init_send.at[piece, i],
+                w_recv.at[piece, q, x],
+                device,
+                part_rows,
+            )
+
+    def arrive(piece, source, part):
+        ref = w_at(piece, source, part)
+        remote(
+            ref, ref, init_send.at[0, 0], w_recv.at[piece, source, part], sibling
+        ).wait_recv()
+
+    def relay(piece, source, sem, device):
+        ref = w_at(piece, source, x)
+        return remote(ref, ref, sem, w_recv.at[piece, source, x], device)
+
+    near_sources = [g * A + t for t in (across_y, across_z, across)]
+    far_sources = [(1 - g) * A + t for t in (c, across_y, across_z, across)]
+
+    def pair_relay(piece, i):
+        return relay(piece, (near_sources + far_sources)[i], pair_send.at[piece, i], pair)
+
+    def far_relay(piece, i):
+        return relay(piece, near_sources[i], far_send.at[piece, i], far)
+
+    def near_arrivals(piece):
+        for i, source in enumerate(near_sources):
+            arrive(piece, source, x)
+            far_relay(piece, i).start()
+            pair_relay(piece, i).start()
+
+    def far_arrivals(piece):
+        for i, source in enumerate(far_sources):
+            arrive(piece, source, x)
+            pair_relay(piece, len(near_sources) + i).start()
+
+    def token_rows(side, k):
+        return pl.ds(pl.multiple_of(side * half + k * step, step), step)
+
+    def token_copy(block, k, ssem, rsem, device):
+        ref = normed.at[block, token_rows(d, k)]
+        return remote(ref, ref, ssem, rsem, device)
+
+    def own_copies(k):
+        return (
+            token_copy(c, k, own_send.at[0, k], tok_recv.at[0, k], quad[1]),
+            token_copy(c, k, own_send.at[1, k], tok_recv.at[1, k], quad[0]),
+            token_copy(c, k, own_send.at[2, k], sib_recv.at[3, k], sibling),
+        )
+
+    def pass_copy(k):
+        return token_copy(across_z, k, pass_send.at[k], tok_recv.at[2, k], quad[0])
+
+    token_blocks = (across_z, across_y, across)
+
+    def share_copy(i, k):
+        return token_copy(
+            token_blocks[i], k, share_send.at[i, k], sib_recv.at[i, k], sibling
+        )
+
+    def token_arrival(i, k):
+        ref = normed.at[token_blocks[i], token_rows(d, k)]
+        remote(ref, ref, own_send.at[0, 0], tok_recv.at[i, k], sibling).wait_recv()
+        if i == 0:
+            pass_copy(k).start()
+        share_copy(i, k).start()
+
+    def normalize(k):
+        def block(i, carry):
+            span = pl.ds(pl.multiple_of(k * step + i * 16, 16), 16)
+            into = pl.ds(pl.multiple_of(d * half + k * step + i * 16, 16), 16)
+            inputs = tokraw[span].astype(jnp.float32)
+            mean = jnp.mean(inputs * inputs, -1, keepdims=True)
+            normed[c, into] = (inputs * lax.rsqrt(mean + 1e-05) * gain[...]).astype(
+                jnp.bfloat16
+            )
+            return carry
+
+        lax.fori_loop(0, step // 16, block, 0)
+
+    lane = lax.broadcasted_iota(jnp.int32, (rows, HD), 1)
+    row_id = lax.broadcasted_iota(jnp.int32, (rows, 1), 0)
+
+    def make_tables():
+        step_angle = (row_id % blk).astype(jnp.float32) * freq[...]
+        step_cos = jnp.cos(step_angle)
+        step_sin = jnp.sin(step_angle)
+        sign = jnp.where(lane < HD // 2, -1.0, 1.0)
+        entry_id = lax.broadcasted_iota(jnp.int32, (A * slots, 1), 0)
+        entries = jnp.zeros((A * slots, 1), jnp.int32)
+        for k in range(A * slots):
+            entries = jnp.where(entry_id == k, order_ref[g * A * slots + k], entries)
+        base_angle = (entries * blk).astype(jnp.float32) * freq[...]
+        base_cos = jnp.cos(base_angle)
+        base_sin = jnp.sin(base_angle)
+        for b in range(A):
+            row_cos = jnp.broadcast_to(base_cos[b * slots : b * slots + 1], (rows, HD))
+            row_sin = jnp.broadcast_to(base_sin[b * slots : b * slots + 1], (rows, HD))
+            for i in range(1, slots):
+                k = b * slots + i
+                row_cos = jnp.where(row_id // blk == i, base_cos[k : k + 1], row_cos)
+                row_sin = jnp.where(row_id // blk == i, base_sin[k : k + 1], row_sin)
+            csbuf[0, b] = row_cos * step_cos - row_sin * step_sin
+            csbuf[1, b] = (row_sin * step_cos + row_cos * step_sin) * sign
+
+    def make_bias():
+        key_id = lax.broadcasted_iota(jnp.int32, (1, T), 1)
+        key_pos = jnp.zeros((1, T), jnp.int32)
+        key_doc = jnp.zeros((1, T), jnp.int32)
+        for i in range(T // blk):
+            here = key_id // blk == i
+            natural = order_ref[i]
+            key_pos = jnp.where(here, natural * blk, key_pos)
+            key_doc = jnp.where(here, docs_ref[natural], key_doc)
+        key_pos = key_pos + key_id % blk
+
+        def block(b, carry):
+            first = jnp.zeros((rows, 1), jnp.int32)
+            document = jnp.zeros((rows, 1), jnp.int32)
+            for i in range(slots):
+                natural = order_ref[(g * A + b) * slots + i]
+                here = row_id // blk == i
+                first = jnp.where(here, natural * blk, first)
+                document = jnp.where(here, docs_ref[natural], document)
+            allowed = (key_pos <= first + row_id % blk) & (key_doc == document)
+            bias[b] = jnp.where(allowed, 0.0, -jnp.inf)
+            return carry
+
+        lax.fori_loop(0, A, block, 0)
+
+    def pick_copies():
+        mine = heads // 2
+        count = picked.shape[1]
+        into = pl.ds(pl.multiple_of(d * count, count), count)
+        return (
+            pltpu.make_async_copy(picked.at[0], cache_ref.at[into], cache_sem.at[0]),
+            remote(
+                picked.at[1], cache_ref.at[into], cache_sem.at[1], cache_sem.at[2], sibling
+            ),
+        )
+
+    def pick_heads():
+        prev_copy.wait()
+        mine = heads // 2
+        group = HD
+        taken = group // 2
+        out_id = lax.broadcasted_iota(jnp.int32, (taken, group), 0)
+        in_id = lax.broadcasted_iota(jnp.int32, (taken, group), 1)
+        for side in range(2):
+            other = d if side == 0 else 1 - d
+            wanted = jnp.zeros((taken, group), jnp.int32)
+            for s in range(mine):
+                wanted = jnp.where(out_id % mine == s, owner_ref[other * mine + s], wanted)
+            chosen = (out_id // mine == in_id // heads) & (in_id % heads == wanted)
+            selector = jnp.where(chosen, 1.0, 0.0).astype(jnp.bfloat16)
+            for i in range(prev.shape[0] // group):
+                picked[side, i * taken : (i + 1) * taken] = jnp.dot(
+                    selector,
+                    prev[i * group : (i + 1) * group],
+                    preferred_element_type=jnp.float32,
+                ).astype(jnp.bfloat16)
+        for copy in pick_copies():
+            copy.start()
+
+    def turn(v, b):
+        return v * csbuf[0, b] + pltpu.roll(v, HD // 2, 1) * csbuf[1, b]
+
+    def kv_copy(n, side, b, device):
+        ref = kvbuf.at[y, side * A + b]
+        return remote(ref, ref, kv_send.at[n, b], kv_recv.at[n, b], device)
+
+    def kv_arrival(n, unit, side):
+        for b in range(A):
+            ref = kvbuf.at[unit, side * A + b]
+            remote(ref, ref, kv_send.at[0, 0], kv_recv.at[n, b], sibling).wait_recv()
+            if n == 1:
+                kv_copy(2, side, b, quad[0]).start()
+
+    def project_kv(b, carry):
+        raw = jnp.dot(normed[b], wbuf[0], preferred_element_type=jnp.float32)
+        kvbuf[y, g * A + b] = jnp.where(y == 0, turn(raw, b), raw).astype(jnp.bfloat16)
+        kv_copy(1, g, b, far).start()
+        kv_copy(0, g, b, quad[0]).start()
+        return carry
+
+    def span_of(source, part):
+        return pl.ds(pl.multiple_of(source * R + part * Rp, Rp), Rp)
+
+    def partial(piece, b, spans):
+        total = None
+        for span in spans:
+            term = jnp.dot(
+                normed[b, :, span], wbuf[piece, span], preferred_element_type=jnp.float32
+            )
+            total = term if total is None else total + term
+        return total
+
+    scale = 1.0 / math.sqrt(HD)
+
+    def att_copy(h, s, b):
+        cols = pl.ds(pl.multiple_of((c * hpg + h) * HD, HD), HD)
+        return remote(
+            att.at[h, b],
+            out_ref.at[:, cols],
+            att_send.at[h, s],
+            att_recv.at[h, c],
+            dev(x, g * A + b, d),
+        )
+
+    def own_out(h):
+        cols = pl.ds(pl.multiple_of((c * hpg + h) * HD, HD), HD)
+        return pltpu.make_async_copy(att.at[h, c], out_ref.at[:, cols], out_sem.at[h])
+
+    def order(s):
+        back = A - 1 - s
+        return near(back // 2, back % 2)
+
+    def attend(h, s, b, query):
+        scores = (
+            lax.dot_general(
+                query,
+                kvbuf[0].reshape(T, HD),
+                (((1,), (1,)), ((), ())),
+                preferred_element_type=jnp.float32,
+            )
+            * scale
+            + bias[b]
+        )
+        weights = jnp.exp(scores - jnp.max(scores, -1, keepdims=True))
+        total = jnp.sum(weights, -1, keepdims=True)
+        weighted = jnp.dot(
+            weights.astype(jnp.bfloat16),
+            kvbuf[1].reshape(T, HD),
+            preferred_element_type=jnp.float32,
+        )
+        att[h, b] = (weighted / total).astype(jnp.bfloat16)
+
+        @pl.when(s < A - 1)
+        def _():
+            att_copy(h, s, b).start()
+
+    first_sends(0)
+    tok_copy.wait()
+    gain_copy.wait()
+    for k in range(chunks):
+        normalize(k)
+        for copy in own_copies(k):
+            copy.start()
+    freq_copy.wait()
+    make_tables()
+    near_arrivals(0)
+    first_sends(1)
+    make_bias()
+    pick_heads()
+    for k in range(chunks):
+        token_arrival(1, k)
+        token_arrival(0, k)
+    far_arrivals(0)
+    for k in range(chunks):
+        token_arrival(2, k)
+    near_arrivals(1)
+    for piece in range(2, pieces):
+        first_sends(piece)
+    for i, block in enumerate((*token_blocks, c)):
+        for k in range(chunks):
+            ref = normed.at[block, token_rows(1 - d, k)]
+            remote(ref, ref, own_send.at[0, 0], sib_recv.at[i, k], sibling).wait_recv()
+    for piece in range(pieces):
+        pltpu.make_async_copy(own_rows(piece), own_rows(piece), local_sem.at[piece]).wait()
+    for source in near_sources + far_sources:
+        arrive(0, source, 1 - x)
+    lax.fori_loop(0, A, project_kv, 0)
+
+    def project_all(piece):
+        def project(s, carry):
+            b = order(s)
+            product = jnp.dot(normed[b], wbuf[piece], preferred_element_type=jnp.float32)
+            qbuf[b] = turn(product, b).astype(jnp.bfloat16)
+            return carry
+
+        lax.fori_loop(0, A, project, 0)
+
+    for h in range(hpg - 1):
+        far_arrivals(1 + h)
+        near_arrivals(2 + h)
+        for source in near_sources + far_sources:
+            arrive(1 + h, source, 1 - x)
+        project_all(1 + h)
+        if h == 0:
+            kv_arrival(1, y, 1 - g)
+            kv_arrival(0, 1 - y, g)
+        if h == hpg - 2:
+            far_arrivals(2 + h)
+        if h == 0:
+            kv_arrival(2, 1 - y, 1 - g)
+
+        def attend_one(s, carry):
+            b = order(s)
+            attend(h, s, b, qbuf[b])
+            return carry
+
+        lax.fori_loop(0, A, attend_one, 0)
+        own_out(h).start()
+
+    last = hpg - 1
+    early = [span_of(q, 0), span_of(q, 1)]
+    early += [span_of(source, x) for source in near_sources + far_sources]
+
+    def project_early(b, carry):
+        acc[b] = partial(hpg, b, early)
+        return carry
+
+    lax.fori_loop(0, A, project_early, 0)
+    for source in near_sources:
+        arrive(hpg, source, 1 - x)
+    middle = [span_of(source, 1 - x) for source in near_sources]
+
+    def project_middle(b, carry):
+        acc[b] += partial(hpg, b, middle)
+        return carry
+
+    lax.fori_loop(0, A, project_middle, 0)
+    for source in far_sources:
+        arrive(hpg, source, 1 - x)
+    late = [span_of(source, 1 - x) for source in far_sources]
+
+    def attend_last(s, carry):
+        b = order(s)
+        product = acc[b] + partial(hpg, b, late)
+        attend(last, s, b, turn(product, b).astype(jnp.bfloat16))
+        return carry
+
+    lax.fori_loop(0, A, attend_last, 0)
+    own_out(last).start()
+
+    for piece in range(pieces):
+        for i in range(A):
+            ref = w_at(piece, q, x)
+            remote(
+                ref, ref, init_send.at[piece, i], w_recv.at[piece, q, x], far
+            ).wait_send()
+        for i in range(len(near_sources)):
+            far_relay(piece, i).wait_send()
+        for i in range(len(near_sources) + len(far_sources)):
+            pair_relay(piece, i).wait_send()
+    for k in range(chunks):
+        for copy in own_copies(k):
+            copy.wait_send()
+        pass_copy(k).wait_send()
+        for i in range(len(token_blocks)):
+            share_copy(i, k).wait_send()
+    for b in range(A):
+        kv_copy(0, g, b, quad[0]).wait_send()
+        kv_copy(1, g, b, far).wait_send()
+        kv_copy(2, 1 - g, b, quad[0]).wait_send()
+    local_pick, sent_pick = pick_copies()
+    local_pick.wait()
+    sent_pick.wait()
+    for h in range(hpg):
+        own_out(h).wait()
+        for s in range(A - 1):
+            att_copy(h, s, order(s)).wait_send()
+        for t in (across, across_z, across_y):
+            cols = pl.ds(pl.multiple_of((t * hpg + h) * HD, HD), HD)
+            remote(
+                att.at[h, 0], out_ref.at[:, cols], att_send.at[h, 0], att_recv.at[h, t], sibling
+            ).wait_recv()
+
+
+def quad_plan(
+    tokens, norm_gain, w_query, w_key, w_value, block_order, block_docs, head_owner, prev_kv
+):
+    n_seq = lax.axis_size("seq")
+    rows, width = tokens.shape
+    R = w_query.shape[0]
+    local_kv = w_key.shape[1] // HD
+    local_heads = w_query.shape[1] // HD
+    A = 2 * local_kv
+    hpg = local_heads // A
+    slots = block_order.shape[0] // n_seq
+    blk = rows // slots
+    T = n_seq * rows
+    chunks = 2
+    kept, planes, heads, _ = prev_kv.shape
+    count = kept * planes * (heads // 2)
+    frequency = 500000.0 ** (-np.arange(HD // 2, dtype=np.float64) / (HD // 2))
+    freq = np.concatenate([frequency, frequency]).astype(np.float32)[None, :]
+    sizes = (A, rows, R, hpg, slots, blk, T, chunks, heads)
+    pieces = hpg + 1
+    dma = pltpu.SemaphoreType.DMA
+    smem = pl.BlockSpec(memory_space=pltpu.SMEM)
+    anywhere = pl.BlockSpec(memory_space=pl.ANY)
+    bf16, f32 = jnp.bfloat16, jnp.float32
+    attended, cache = pl.pallas_call(
+        functools.partial(quad_kernel, sizes),
+        out_shape=(
+            jax.ShapeDtypeStruct((rows, local_heads * HD), bf16),
+            jax.ShapeDtypeStruct((2 * count, HD), prev_kv.dtype),
+        ),
+        in_specs=[smem] * 3 + [anywhere] * 7,
+        out_specs=(anywhere, anywhere),
+        scratch_shapes=[
+            pltpu.VMEM((1, HD), f32),
+            pltpu.VMEM((1, width), f32),
+            pltpu.VMEM((rows // 2, width), bf16),
+            pltpu.VMEM((pieces, width, HD), bf16),
+            pltpu.VMEM((A, rows, width), bf16),
+            pltpu.VMEM((A, rows, HD), bf16),
+            pltpu.VMEM((A, rows, HD), f32),
+            pltpu.VMEM((2, n_seq, rows, HD), bf16),
+            pltpu.VMEM((2, A, rows, HD), f32),
+            pltpu.VMEM((A, rows, T), f32),
+            pltpu.VMEM((hpg, A, rows, HD), bf16),
+            pltpu.VMEM((kept * planes * heads, HD), bf16),
+            pltpu.VMEM((2, count, HD), bf16),
+            dma((pieces + 4,)),
+            dma((pieces, A)),
+            dma((pieces, A - 1)),
+            dma((pieces, n_seq - 1)),
+            dma((pieces, n_seq, 2)),
+            dma((3, chunks)),
+            dma((chunks,)),
+            dma((3, chunks)),
+            dma((3, chunks)),
+            dma((4, chunks)),
+            dma((3, A)),
+            dma((3, A)),
+            dma((hpg, A)),
+            dma((hpg, A)),
+            dma((hpg,)),
+            dma((3,)),
+        ],
+        compiler_params=pltpu.CompilerParams(collective_id=1, has_side_effects=True),
+    )(
+        block_order,
+        block_docs,
+        head_owner,
+        freq,
+        norm_gain[None, :],
+        tokens,
+        w_query,
+        w_key,
+        w_value,
+        prev_kv.reshape(kept * planes * heads, HD),
+    )
+    return attended, cache.reshape(2 * kept, planes, heads // 2, HD)
+
+
 def solution(mesh):
     in_specs = (
         P(("groups", "seq"), None),
@@ -691,7 +1276,19 @@
             and w_query.shape[0] % (16 * X) == 0
             and tokens.shape[0] % 32 == 0
         )
+        squared = (
+            fits
+            and A == 4
+            and X == 2
+            and n_seq == 2 * A
+            and heads >= 2 * A
+            and tokens.shape[0] % 128 == 0
+            and rest[-1].shape[3] == HD
+            and HD % (2 * rest[-1].shape[2]) == 0
+            and (rest[-1].shape[0] * rest[-1].shape[1] * rest[-1].shape[2]) % HD == 0
+        )
         plan = functools.partial(column_plan, X) if fits else general_plan
+        plan = quad_plan if squared else plan
         return plan(tokens, norm_gain, w_query, w_key, w_value, *rest)
 
     return jax.shard_map(

time: 87.2 us -> 76.9 us (0.88)
  between operations: 4.71 us -> 0.65 us
  Pallas kernels: 77.1 us -> 73.7 us
  other arithmetic: 3.04 us -> 0 us
    pallas_call x1, Pallas kernels: 77.1 us -> 73.7 us  [quad_plan(): pl.pallas_call(functools.partial(quad_kernel, sizes), out_shape=(jax.Shap...]
    select_n x2 -> x0, other arithmetic: 1.48 us -> none  [the longest x1 0.93 us: column_plan(): jnp.where(d == 0, prev_kv, other)]
    unnamed x7 -> x4, local copies, waits for them, and re-layouts: 1.36 us -> 2.36 us
    another operation x1 -> x0, other arithmetic: 0.96 us -> none  [column_plan(): return (attended, jnp.stack(picks, 2))]
where the time goes in v1:
time: 76.9 us; the launch traced here: 76.7 us
  Pallas kernels  73.7 us (96%)
  local copies, waits for them, and re-layouts  2.36 us (3%)
    pallas_call x1, Pallas kernels, quad_plan(): pl.pallas_call(functools.partial(quad_kernel, sizes), out_shape=(jax.Shap...  73.7 us
    unnamed x4, local copies, waits for them, and re-layouts  2.36 us

profile of v1, /device:TPU:0, one launch (start us, length us, event | category | flops | bytes accessed | tf_op | source)
XLA Modules:
  0.0 76.7 jit_solution(726558266221195785)
XLA Ops:
  0.6 73.7 %shard_map.113 = (bf16[128,1024]{1,0:T(8,128)(2,1)}, bf16[512,128]{1,0:T(8,128)(2,1)}) custom-call(s32[16]{0:T(128)} %order_ref.1, s32[16]{0:T(128)} %docs_ref.1, s32[4]{0:T(128)} %owner_ref.1, f32[1,128]{1,0:T(1,128)} %constant.2.clone.freq_in, f32[1,4096]{1,0:T(1,128)} %bitcast.5, bf16[128,4096]{1,0:T(8,128)(2,1)} %tok_in.1, bf16[512,1024]{1,0:T(8,128)(2,1)} %wq_in.1, ...), custom_call_target="tpu_custom_call" | custom-call | tf_op jit(solution)/shard_map/pallas_call | solution.py:1197
  74.4 0.0 copy-start
  74.4 1.7 %copy.14 = bf16[128,1024]{1,0:T(8,128)(2,1)} copy(bf16[128,1024]{1,0:T(8,128)(2,1)} %get-tuple-element.8) | data formatting | bytes 524288
  76.1 0.0 copy-done
  76.1 0.7 copy.15
Async XLA Ops:
  74.4 1.7 %copy-start = (bf16[512,128]{1,0:T(8,128)(2,1)S(1)}, bf16[512,128]{1,0:T(8,128)(2,1)}, u32[]{:S(2)}) copy-start(bf16[512,128]{1,0:T(8,128)(2,1)} %get-tuple-element.5) | copy-start | bytes 393220

commit v2 on v1

--- a/solution.py
+++ b/solution.py
@@ -665,7 +665,22 @@
     return attended, jnp.stack(picks, 2)
 
 
+PLAN = (
+    ("first", 0, 2), ("first", 1, 2), ("first", 2, 3), ("first", 0, 3), ("first", 1, 3),
+    ("first", 1, 0), ("first", 1, 1), ("first", 0, 1), ("near", 2, 0), ("near", 0, 1),
+    ("far", 1, 0), ("spare", 0), ("spare", 1), ("own", 1), ("own", 0), ("near", 0, 0),
+    ("far", 2, 1), ("first", 0, 0), ("near", 1, 0), ("near", 0, 2), ("near", 1, 1),
+    ("far", 0, 2), ("tok", 0, 1), ("tok", 0, 0), ("first", 2, 2), ("tok", 1, 0),
+    ("far", 0, 0), ("first", 2, 0), ("far", 0, 1), ("far", 0, 3), ("tok", 2, 1),
+    ("near", 1, 2), ("near", 2, 1), ("far", 1, 2), ("far", 1, 1), ("tok", 1, 1),
+    ("tok", 2, 0), ("first", 2, 1), ("keys",), ("far", 1, 3), ("far", 2, 0), ("kv", 0),
+    ("near", 2, 2), ("far", 2, 2), ("kv", 1), ("query",), ("far", 2, 3), ("early",),
+    ("kv", 2), ("head",), ("last",),
+)
+
+
 def quad_kernel(
+    plan,
     sizes,
     order_ref,
     docs_ref,
@@ -794,18 +809,19 @@
         pl.semaphore_signal(barrier, inc=1, device_id=peer, device_id_type=pl.DeviceIdType.MESH)
     pl.semaphore_wait(barrier, len(peers))
 
-    def first_sends(piece):
-        targets = [(c, far), (across, quad[2]), (across_z, quad[1]), (across_y, quad[0])]
-        for i, (t, device) in enumerate(targets):
-            start_weights(
-                piece,
-                t,
-                w_at(piece, q, x),
-                init_send.at[piece, i],
-                w_recv.at[piece, q, x],
-                device,
-                part_rows,
-            )
+    targets = ((c, far), (across, quad[2]), (across_z, quad[1]), (across_y, quad[0]))
+
+    def first_send(piece, i):
+        t, device = targets[i]
+        start_weights(
+            piece,
+            t,
+            w_at(piece, q, x),
+            init_send.at[piece, i],
+            w_recv.at[piece, q, x],
+            device,
+            part_rows,
+        )
 
     def arrive(piece, source, part):
         ref = w_at(piece, source, part)
@@ -826,16 +842,14 @@
     def far_relay(piece, i):
         return relay(piece, near_sources[i], far_send.at[piece, i], far)
 
-    def near_arrivals(piece):
-        for i, source in enumerate(near_sources):
-            arrive(piece, source, x)
-            far_relay(piece, i).start()
-            pair_relay(piece, i).start()
-
-    def far_arrivals(piece):
-        for i, source in enumerate(far_sources):
-            arrive(piece, source, x)
-            pair_relay(piece, len(near_sources) + i).start()
+    def near_arrival(piece, i):
+        arrive(piece, near_sources[i], x)
+        far_relay(piece, i).start()
+        pair_relay(piece, i).start()
+
+    def far_arrival(piece, i):
+        arrive(piece, far_sources[i], x)
+        pair_relay(piece, len(near_sources) + i).start()
 
     def token_rows(side, k):
         return pl.ds(pl.multiple_of(side * half + k * step, step), step)
@@ -1042,99 +1056,112 @@
         def _():
             att_copy(h, s, b).start()
 
-    first_sends(0)
-    tok_copy.wait()
-    gain_copy.wait()
-    for k in range(chunks):
+    def own_tokens(k):
+        if k == plan[0]:
+            tok_copy.wait()
+            gain_copy.wait()
         normalize(k)
         for copy in own_copies(k):
             copy.start()
-    freq_copy.wait()
-    make_tables()
-    near_arrivals(0)
-    first_sends(1)
-    make_bias()
-    pick_heads()
-    for k in range(chunks):
-        token_arrival(1, k)
-        token_arrival(0, k)
-    far_arrivals(0)
-    for k in range(chunks):
-        token_arrival(2, k)
-    near_arrivals(1)
-    for piece in range(2, pieces):
-        first_sends(piece)
-    for i, block in enumerate((*token_blocks, c)):
-        for k in range(chunks):
-            ref = normed.at[block, token_rows(1 - d, k)]
-            remote(ref, ref, own_send.at[0, 0], sib_recv.at[i, k], sibling).wait_recv()
-    for piece in range(pieces):
-        pltpu.make_async_copy(own_rows(piece), own_rows(piece), local_sem.at[piece]).wait()
-    for source in near_sources + far_sources:
-        arrive(0, source, 1 - x)
-    lax.fori_loop(0, A, project_kv, 0)
-
-    def project_all(piece):
+
+    def spare(i):
+        if i:
+            make_bias()
+            pick_heads()
+        else:
+            freq_copy.wait()
+            make_tables()
+
+    def start_keys():
+        for i, block in enumerate((*token_blocks, c)):
+            for k in range(chunks):
+                ref = normed.at[block, token_rows(1 - d, k)]
+                remote(
+                    ref, ref, own_send.at[0, 0], sib_recv.at[i, k], sibling
+                ).wait_recv()
+        for piece in range(pieces):
+            pltpu.make_async_copy(
+                own_rows(piece), own_rows(piece), local_sem.at[piece]
+            ).wait()
+        for source in near_sources + far_sources:
+            arrive(0, source, 1 - x)
+        lax.fori_loop(0, A, project_kv, 0)
+
+    def project_first():
+        for source in near_sources + far_sources:
+            arrive(1, source, 1 - x)
+
         def project(s, carry):
             b = order(s)
-            product = jnp.dot(normed[b], wbuf[piece], preferred_element_type=jnp.float32)
+            product = jnp.dot(normed[b], wbuf[1], preferred_element_type=jnp.float32)
             qbuf[b] = turn(product, b).astype(jnp.bfloat16)
             return carry
 
         lax.fori_loop(0, A, project, 0)
 
-    for h in range(hpg - 1):
-        far_arrivals(1 + h)
-        near_arrivals(2 + h)
-        for source in near_sources + far_sources:
-            arrive(1 + h, source, 1 - x)
-        project_all(1 + h)
-        if h == 0:
-            kv_arrival(1, y, 1 - g)
-            kv_arrival(0, 1 - y, g)
-        if h == hpg - 2:
-            far_arrivals(2 + h)
-        if h == 0:
-            kv_arrival(2, 1 - y, 1 - g)
-
+    def attend_first():
         def attend_one(s, carry):
             b = order(s)
-            attend(h, s, b, qbuf[b])
+            attend(0, s, b, qbuf[b])
             return carry
 
         lax.fori_loop(0, A, attend_one, 0)
-        own_out(h).start()
-
-    last = hpg - 1
-    early = [span_of(q, 0), span_of(q, 1)]
-    early += [span_of(source, x) for source in near_sources + far_sources]
-
-    def project_early(b, carry):
-        acc[b] = partial(hpg, b, early)
-        return carry
-
-    lax.fori_loop(0, A, project_early, 0)
-    for source in near_sources:
-        arrive(hpg, source, 1 - x)
-    middle = [span_of(source, 1 - x) for source in near_sources]
-
-    def project_middle(b, carry):
-        acc[b] += partial(hpg, b, middle)
-        return carry
-
-    lax.fori_loop(0, A, project_middle, 0)
-    for source in far_sources:
-        arrive(hpg, source, 1 - x)
-    late = [span_of(source, 1 - x) for source in far_sources]
-
-    def attend_last(s, carry):
-        b = order(s)
-        product = acc[b] + partial(hpg, b, late)
-        attend(last, s, b, turn(product, b).astype(jnp.bfloat16))
-        return carry
-
-    lax.fori_loop(0, A, attend_last, 0)
-    own_out(last).start()
+        own_out(0).start()
+
+    def kv_arrivals(n):
+        kv_arrival(n, *((1 - y, g), (y, 1 - g), (1 - y, 1 - g))[n])
+
+    last = hpg
+
+    def project_early():
+        early = [span_of(q, 0), span_of(q, 1)]
+        early += [span_of(source, x) for source in near_sources + far_sources]
+
+        def project(b, carry):
+            acc[b] = partial(last, b, early)
+            return carry
+
+        lax.fori_loop(0, A, project, 0)
+
+    def attend_last():
+        for source in near_sources:
+            arrive(last, source, 1 - x)
+        middle = [span_of(source, 1 - x) for source in near_sources]
+
+        def project(b, carry):
+            acc[b] += partial(last, b, middle)
+            return carry
+
+        lax.fori_loop(0, A, project, 0)
+        for source in far_sources:
+            arrive(last, source, 1 - x)
+        late = [span_of(source, 1 - x) for source in far_sources]
+
+        def attend_one(s, carry):
+            b = order(s)
+            product = acc[b] + partial(last, b, late)
+            attend(1, s, b, turn(product, b).astype(jnp.bfloat16))
+            return carry
+
+        lax.fori_loop(0, A, attend_one, 0)
+        own_out(1).start()
+
+    steps = {
+        "first": first_send,
+        "near": near_arrival,
+        "far": far_arrival,
+        "own": own_tokens,
+        "tok": token_arrival,
+        "spare": spare,
+        "keys": start_keys,
+        "kv": kv_arrivals,
+        "query": project_first,
+        "head": attend_first,
+        "early": project_early,
+        "last": attend_last,
+    }
+    for name, *where in plan[1]:
+        steps[name](*where)
 
     for piece in range(pieces):
         for i in range(A):
@@ -1183,7 +1210,8 @@
     slots = block_order.shape[0] // n_seq
     blk = rows // slots
     T = n_seq * rows
-    chunks = 2
+    owned = [where[0] for name, *where in PLAN if name == "own"]
+    first_own, chunks = owned[0], len(owned)
     kept, planes, heads, _ = prev_kv.shape
     count = kept * planes * (heads // 2)
     frequency = 500000.0 ** (-np.arange(HD // 2, dtype=np.float64) / (HD // 2))
@@ -1195,10 +1223,10 @@
     anywhere = pl.BlockSpec(memory_space=pl.ANY)
     bf16, f32 = jnp.bfloat16, jnp.float32
     attended, cache = pl.pallas_call(
-        functools.partial(quad_kernel, sizes),
+        functools.partial(quad_kernel, (first_own, PLAN), sizes),
         out_shape=(
-            jax.ShapeDtypeStruct((rows, local_heads * HD), bf16),
-            jax.ShapeDtypeStruct((2 * count, HD), prev_kv.dtype),
+            pltpu.VMEM((rows, local_heads * HD), bf16),
+            pltpu.VMEM((2 * count, HD), prev_kv.dtype),
         ),
         in_specs=[smem] * 3 + [anywhere] * 7,
         out_specs=(anywhere, anywhere),
@@ -1281,7 +1309,7 @@
             and A == 4
             and X == 2
             and n_seq == 2 * A
-            and heads >= 2 * A
+            and heads == 2 * A
             and tokens.shape[0] % 128 == 0
             and rest[-1].shape[3] == HD
             and HD % (2 * rest[-1].shape[2]) == 0

time: 76.9 us -> 66.7 us (0.87)
  Pallas kernels: 73.7 us -> 64.5 us
  local copies, waits for them, and re-layouts: 2.36 us -> 1.36 us
    pallas_call x1, Pallas kernels: 73.7 us -> 64.5 us  [quad_plan(): pl.pallas_call(functools.partial(quad_kernel, (first_own, PLAN), sizes),...]
    unnamed x4 -> x2, local copies, waits for them, and re-layouts: 2.36 us -> 1.36 us
where the time goes in v2:
time: 66.7 us; the launch traced here: 66.5 us
  Pallas kernels  64.5 us (97%)
  local copies, waits for them, and re-layouts  1.36 us (2%)
    pallas_call x1, Pallas kernels, quad_plan(): pl.pallas_call(functools.partial(quad_kernel, (first_own, PLAN), sizes),...  64.5 us
    unnamed x2, local copies, waits for them, and re-layouts  1.36 us

profile of v2, /device:TPU:0, one launch (start us, length us, event | category | flops | bytes accessed | tf_op | source)
XLA Modules:
  0.0 66.5 jit_solution(9510690615575823267)
XLA Ops:
  0.6 64.5 %shard_map.113 = (bf16[128,1024]{1,0:T(8,128)(2,1)S(1)}, bf16[512,128]{1,0:T(8,128)(2,1)S(1)}) custom-call(s32[16]{0:T(128)} %order_ref.1, s32[16]{0:T(128)} %docs_ref.1, s32[4]{0:T(128)} %owner_ref.1, f32[1,128]{1,0:T(1,128)} %constant.2.clone.freq_in, f32[1,4096]{1,0:T(1,128)} %bitcast.5, bf16[128,4096]{1,0:T(8,128)(2,1)} %tok_in.1, ...), custom_call_target="tpu_custom_call" | custom-call | tf_op jit(solution)/shard_map/pallas_call | solution.py:1225
  65.2 0.7 %copy.14 = bf16[128,1024]{1,0:T(8,128)(2,1)} copy(bf16[128,1024]{1,0:T(8,128)(2,1)S(1)} %get-tuple-element.6) | data formatting | bytes 524288
  65.9 0.7 copy.15

commit v3 on v2

--- a/solution.py
+++ b/solution.py
@@ -666,25 +666,26 @@
 
 
 PLAN = (
-    ("first", 0, 2), ("first", 1, 2), ("first", 2, 3), ("first", 0, 3), ("first", 1, 3),
-    ("first", 1, 0), ("first", 1, 1), ("first", 0, 1), ("near", 2, 0), ("near", 0, 1),
-    ("far", 1, 0), ("spare", 0), ("spare", 1), ("own", 1), ("own", 0), ("near", 0, 0),
-    ("far", 2, 1), ("first", 0, 0), ("near", 1, 0), ("near", 0, 2), ("near", 1, 1),
-    ("far", 0, 2), ("tok", 0, 1), ("tok", 0, 0), ("first", 2, 2), ("tok", 1, 0),
-    ("far", 0, 0), ("first", 2, 0), ("far", 0, 1), ("far", 0, 3), ("tok", 2, 1),
-    ("near", 1, 2), ("near", 2, 1), ("far", 1, 2), ("far", 1, 1), ("tok", 1, 1),
-    ("tok", 2, 0), ("first", 2, 1), ("keys",), ("far", 1, 3), ("far", 2, 0), ("kv", 0),
-    ("near", 2, 2), ("far", 2, 2), ("kv", 1), ("query",), ("far", 2, 3), ("early",),
-    ("kv", 2), ("head",), ("last",),
+    ("first", 0, 2), ("first", 1, 1), ("spare", 1), ("first", 0, 1), ("first", 1, 0),
+    ("first", 2, 3), ("first", 0, 3), ("first", 1, 2), ("own", 2), ("near", 2, 0), ("own", 1),
+    ("first", 0, 0), ("near", 0, 2), ("own", 0), ("near", 0, 1), ("tok", 0, 2), ("tok", 1, 2),
+    ("near", 1, 2), ("own", 3), ("far", 0, 3), ("tok", 2, 2), ("first", 1, 3), ("near", 0, 0),
+    ("tok", 1, 1), ("tok", 0, 1), ("near", 1, 1), ("tok", 0, 0), ("far", 0, 0), ("spare", 0),
+    ("tok", 1, 0), ("first", 2, 0), ("near", 1, 0), ("first", 2, 2), ("far", 2, 1),
+    ("far", 0, 2), ("far", 1, 0), ("tok", 0, 3), ("tok", 1, 3), ("far", 0, 1), ("near", 2, 1),
+    ("tok", 2, 3), ("tok", 2, 1), ("far", 1, 3), ("tok", 2, 0), ("first", 2, 1),
+    ("far", 1, 1), ("far", 1, 2), ("keys",), ("far", 2, 2), ("near", 2, 2), ("kv", 1),
+    ("kv", 0), ("far", 2, 0), ("query",), ("far", 2, 3), ("early",), ("kv", 2), ("head",),
+    ("last",),
 )
 
 
 def quad_kernel(
     plan,
     sizes,
-    order_ref,
-    docs_ref,
-    owner_ref,
+    order_in,
+    docs_in,
+    owner_in,
     freq_in,
     gain_in,
     tok_in,
@@ -694,6 +695,10 @@
     prev_in,
     out_ref,
     cache_ref,
+    order_ref,
+    docs_ref,
+    owner_ref,
+    stage,
     freq,
     gain,
     tokraw,
@@ -708,10 +713,13 @@
     prev,
     picked,
     local_sem,
+    stage_sem,
+    table_sem,
     init_send,
     far_send,
     pair_send,
     w_recv,
+    pair_recv,
     own_send,
     pass_send,
     share_send,
@@ -764,25 +772,10 @@
 
     part_rows = pl.ds(pl.multiple_of(x * Rp, Rp), Rp)
 
-    def start_weights(piece, t, dst, ssem, rsem, device, span):
-        def go(source, column):
-            src = source.at[span, pl.ds(pl.multiple_of(column, HD), HD)]
-            if device is None:
-                pltpu.make_async_copy(src, dst, ssem).start()
-            else:
-                remote(src, dst, ssem, rsem, device).start()
-
+    def weights(piece, t):
         if piece:
-            go(wq_in, (t * hpg + piece - 1) * HD)
-        else:
-
-            @pl.when(t % 2 == 0)
-            def _():
-                go(wk_in, (t // 2) * HD)
-
-            @pl.when(t % 2 == 1)
-            def _():
-                go(wv_in, (t // 2) * HD)
+            return wq_in, (t * hpg + piece - 1) * HD
+        return (wv_in if t % 2 else wk_in), (t // 2) * HD
 
     pieces = hpg + 1
     my_half = pl.ds(pl.multiple_of(d * half, half), half)
@@ -798,10 +791,36 @@
     def own_rows(piece):
         return wbuf.at[piece, pl.ds(pl.multiple_of(q * R, R), R)]
 
+    def own_copy(piece, t):
+        source, column = weights(piece, t)
+        return pltpu.make_async_copy(
+            source.at[:, pl.ds(column, HD)], own_rows(piece), local_sem.at[piece]
+        )
+
+    def stage_copy(piece, t):
+        source, column = weights(piece, t)
+        return pltpu.make_async_copy(
+            source.at[part_rows, pl.ds(column, HD)],
+            stage.at[piece, t],
+            stage_sem.at[piece],
+        )
+
     for piece in range(pieces):
-        start_weights(
-            piece, c, own_rows(piece), local_sem.at[piece], None, None, pl.ds(0, R)
-        )
+        for t in range(A):
+            stage_copy(piece, t).start()
+
+            @pl.when(c == t)
+            def _():
+                own_copy(piece, t).start()
+
+    table_copies = [
+        pltpu.make_async_copy(source, into, table_sem.at[i])
+        for i, (source, into) in enumerate(
+            ((order_in, order_ref), (docs_in, docs_ref), (owner_in, owner_ref))
+        )
+    ]
+    for copy in table_copies:
+        copy.start()
 
     barrier = pltpu.get_barrier_semaphore()
     peers = quad + [far, pair, sibling]
@@ -811,45 +830,56 @@
 
     targets = ((c, far), (across, quad[2]), (across_z, quad[1]), (across_y, quad[0]))
 
+    for piece in range(pieces):
+        pltpu.make_async_copy(stage.at[piece], stage.at[piece], stage_sem.at[piece]).wait()
+
     def first_send(piece, i):
         t, device = targets[i]
-        start_weights(
-            piece,
-            t,
+        remote(
+            stage.at[piece, t],
             w_at(piece, q, x),
-            init_send.at[piece, i],
-            w_recv.at[piece, q, x],
+            init_send.at[piece],
+            w_recv.at[piece, q],
             device,
-            part_rows,
-        )
-
-    def arrive(piece, source, part):
-        ref = w_at(piece, source, part)
-        remote(
-            ref, ref, init_send.at[0, 0], w_recv.at[piece, source, part], sibling
-        ).wait_recv()
-
-    def relay(piece, source, sem, device):
+        ).start()
+
+    def arrive(piece, source):
         ref = w_at(piece, source, x)
-        return remote(ref, ref, sem, w_recv.at[piece, source, x], device)
+        remote(ref, ref, init_send.at[0], w_recv.at[piece, source], sibling).wait_recv()
+
+    def relay(piece, source, ssem, rsem, device):
+        ref = w_at(piece, source, x)
+        return remote(ref, ref, ssem, rsem, device)
+
+    def some_rows(piece, count):
+        return wbuf.at[piece, pl.ds(0, count * Rp)]
+
+    def arrive_pair(piece, group, count):
+        ref = some_rows(piece, count)
+        remote(ref, ref, init_send.at[0], pair_recv.at[piece, group], sibling).wait_recv()
 
     near_sources = [g * A + t for t in (across_y, across_z, across)]
     far_sources = [(1 - g) * A + t for t in (c, across_y, across_z, across)]
 
     def pair_relay(piece, i):
-        return relay(piece, (near_sources + far_sources)[i], pair_send.at[piece, i], pair)
-
-    def far_relay(piece, i):
-        return relay(piece, near_sources[i], far_send.at[piece, i], far)
+        group = int(piece == pieces - 1 and i >= len(near_sources))
+        relay(
+            piece,
+            (near_sources + far_sources)[i],
+            pair_send.at[piece],
+            pair_recv.at[piece, group],
+            pair,
+        ).start()
 
     def near_arrival(piece, i):
-        arrive(piece, near_sources[i], x)
-        far_relay(piece, i).start()
-        pair_relay(piece, i).start()
+        source = near_sources[i]
+        arrive(piece, source)
+        relay(piece, source, far_send.at[piece], w_recv.at[piece, source], far).start()
+        pair_relay(piece, i)
 
     def far_arrival(piece, i):
-        arrive(piece, far_sources[i], x)
-        pair_relay(piece, len(near_sources) + i).start()
+        arrive(piece, far_sources[i])
+        pair_relay(piece, len(near_sources) + i)
 
     def token_rows(side, k):
         return pl.ds(pl.multiple_of(side * half + k * step, step), step)
@@ -860,24 +890,24 @@
 
     def own_copies(k):
         return (
-            token_copy(c, k, own_send.at[0, k], tok_recv.at[0, k], quad[1]),
-            token_copy(c, k, own_send.at[1, k], tok_recv.at[1, k], quad[0]),
-            token_copy(c, k, own_send.at[2, k], sib_recv.at[3, k], sibling),
+            token_copy(c, k, own_send.at[0], tok_recv.at[0, k], quad[1]),
+            token_copy(c, k, own_send.at[1], tok_recv.at[1, k], quad[0]),
+            token_copy(c, k, own_send.at[2], sib_recv.at[0], sibling),
         )
 
     def pass_copy(k):
-        return token_copy(across_z, k, pass_send.at[k], tok_recv.at[2, k], quad[0])
+        return token_copy(across_z, k, pass_send.at[0], tok_recv.at[2, k], quad[0])
 
     token_blocks = (across_z, across_y, across)
 
     def share_copy(i, k):
         return token_copy(
-            token_blocks[i], k, share_send.at[i, k], sib_recv.at[i, k], sibling
+            token_blocks[i], k, share_send.at[i], sib_recv.at[0], sibling
         )
 
     def token_arrival(i, k):
         ref = normed.at[token_blocks[i], token_rows(d, k)]
-        remote(ref, ref, own_send.at[0, 0], tok_recv.at[i, k], sibling).wait_recv()
+        remote(ref, ref, own_send.at[0], tok_recv.at[i, k], sibling).wait_recv()
         if i == 0:
             pass_copy(k).start()
         share_copy(i, k).start()
@@ -984,14 +1014,21 @@
 
     def kv_copy(n, side, b, device):
         ref = kvbuf.at[y, side * A + b]
-        return remote(ref, ref, kv_send.at[n, b], kv_recv.at[n, b], device)
-
-    def kv_arrival(n, unit, side):
-        for b in range(A):
-            ref = kvbuf.at[unit, side * A + b]
-            remote(ref, ref, kv_send.at[0, 0], kv_recv.at[n, b], sibling).wait_recv()
-            if n == 1:
-                kv_copy(2, side, b, quad[0]).start()
+        rsem = kv_recv.at[b] if n == 1 else kv_recv.at[A + n // 2]
+        return remote(ref, ref, kv_send.at[n], rsem, device)
+
+    def kv_arrivals(n):
+        if n == 1:
+            for b in range(A):
+                ref = kvbuf.at[y, (1 - g) * A + b]
+                remote(ref, ref, kv_send.at[0], kv_recv.at[b], sibling).wait_recv()
+                kv_copy(2, 1 - g, b, quad[0]).start()
+        else:
+            side = g if n == 0 else 1 - g
+            ref = kvbuf.at[1 - y, pl.ds(pl.multiple_of(side * A, A), A)]
+            remote(
+                ref, ref, kv_send.at[0], kv_recv.at[A + n // 2], sibling
+            ).wait_recv()
 
     def project_kv(b, carry):
         raw = jnp.dot(normed[b], wbuf[0], preferred_element_type=jnp.float32)
@@ -1014,13 +1051,13 @@
 
     scale = 1.0 / math.sqrt(HD)
 
-    def att_copy(h, s, b):
+    def att_copy(h, b):
         cols = pl.ds(pl.multiple_of((c * hpg + h) * HD, HD), HD)
         return remote(
             att.at[h, b],
             out_ref.at[:, cols],
-            att_send.at[h, s],
-            att_recv.at[h, c],
+            att_send.at[h],
+            att_recv.at[0],
             dev(x, g * A + b, d),
         )
 
@@ -1032,17 +1069,13 @@
         back = A - 1 - s
         return near(back // 2, back % 2)
 
-    def attend(h, s, b, query):
-        scores = (
-            lax.dot_general(
-                query,
-                kvbuf[0].reshape(T, HD),
-                (((1,), (1,)), ((), ())),
-                preferred_element_type=jnp.float32,
-            )
-            * scale
-            + bias[b]
-        )
+    def attend(h, pair_id, blocks, queries):
+        scores = lax.dot_general(
+            jnp.concatenate(queries, 0),
+            kvbuf[0].reshape(T, HD),
+            (((1,), (1,)), ((), ())),
+            preferred_element_type=jnp.float32,
+        ) * scale + jnp.concatenate([bias[b] for b in blocks], 0)
         weights = jnp.exp(scores - jnp.max(scores, -1, keepdims=True))
         total = jnp.sum(weights, -1, keepdims=True)
         weighted = jnp.dot(
@@ -1050,11 +1083,23 @@
             kvbuf[1].reshape(T, HD),
             preferred_element_type=jnp.float32,
         )
-        att[h, b] = (weighted / total).astype(jnp.bfloat16)
-
-        @pl.when(s < A - 1)
+        done = (weighted / total).astype(jnp.bfloat16)
+        for i, b in enumerate(blocks):
+            att[h, b] = done[i * rows : (i + 1) * rows]
+        att_copy(h, blocks[0]).start()
+
+        @pl.when(pair_id < A // 2 - 1)
         def _():
-            att_copy(h, s, b).start()
+            att_copy(h, blocks[1]).start()
+
+    def attend_all(h, query):
+        def attend_pair(s, carry):
+            blocks = [order(2 * s), order(2 * s + 1)]
+            attend(h, s, blocks, [query(b) for b in blocks])
+            return carry
+
+        lax.fori_loop(0, A // 2, attend_pair, 0)
+        own_out(h).start()
 
     def own_tokens(k):
         if k == plan[0]:
@@ -1065,6 +1110,9 @@
             copy.start()
 
     def spare(i):
+        if i == first_spare:
+            for copy in table_copies:
+                copy.wait()
         if i:
             make_bias()
             pick_heads()
@@ -1073,23 +1121,17 @@
             make_tables()
 
     def start_keys():
-        for i, block in enumerate((*token_blocks, c)):
-            for k in range(chunks):
-                ref = normed.at[block, token_rows(1 - d, k)]
-                remote(
-                    ref, ref, own_send.at[0, 0], sib_recv.at[i, k], sibling
-                ).wait_recv()
+        ref = normed.at[pl.ds(0, A // 2)]
+        remote(ref, ref, own_send.at[0], sib_recv.at[0], sibling).wait_recv()
         for piece in range(pieces):
             pltpu.make_async_copy(
                 own_rows(piece), own_rows(piece), local_sem.at[piece]
             ).wait()
-        for source in near_sources + far_sources:
-            arrive(0, source, 1 - x)
+        arrive_pair(0, 0, len(near_sources) + len(far_sources))
         lax.fori_loop(0, A, project_kv, 0)
 
     def project_first():
-        for source in near_sources + far_sources:
-            arrive(1, source, 1 - x)
+        arrive_pair(1, 0, len(near_sources) + len(far_sources))
 
         def project(s, carry):
             b = order(s)
@@ -1100,22 +1142,14 @@
         lax.fori_loop(0, A, project, 0)
 
     def attend_first():
-        def attend_one(s, carry):
-            b = order(s)
-            attend(0, s, b, qbuf[b])
-            return carry
-
-        lax.fori_loop(0, A, attend_one, 0)
-        own_out(0).start()
-
-    def kv_arrivals(n):
-        kv_arrival(n, *((1 - y, g), (y, 1 - g), (1 - y, 1 - g))[n])
+        attend_all(0, lambda b: qbuf[b])
 
     last = hpg
+    near_count, far_count = len(near_sources), len(far_sources)
 
     def project_early():
         early = [span_of(q, 0), span_of(q, 1)]
-        early += [span_of(source, x) for source in near_sources + far_sources]
+        early += [span_of(source, x) for source in near_sources]
 
         def project(b, carry):
             acc[b] = partial(last, b, early)
@@ -1124,27 +1158,22 @@
         lax.fori_loop(0, A, project, 0)
 
     def attend_last():
-        for source in near_sources:
-            arrive(last, source, 1 - x)
+        arrive_pair(last, 0, near_count)
         middle = [span_of(source, 1 - x) for source in near_sources]
+        middle += [span_of(source, x) for source in far_sources]
 
         def project(b, carry):
             acc[b] += partial(last, b, middle)
             return carry
 
         lax.fori_loop(0, A, project, 0)
-        for source in far_sources:
-            arrive(last, source, 1 - x)
+        arrive_pair(last, 1, far_count)
         late = [span_of(source, 1 - x) for source in far_sources]
 
-        def attend_one(s, carry):
-            b = order(s)
-            product = acc[b] + partial(last, b, late)
-            attend(1, s, b, turn(product, b).astype(jnp.bfloat16))
-            return carry
-
-        lax.fori_loop(0, A, attend_one, 0)
-        own_out(1).start()
+        def query(b):
+            return turn(acc[b] + partial(last, b, late), b).astype(jnp.bfloat16)
+
+        attend_all(1, query)
 
     steps = {
         "first": first_send,
@@ -1160,41 +1189,32 @@
         "early": project_early,
         "last": attend_last,
     }
+    first_spare = [where[0] for name, *where in plan[1] if name == "spare"][0]
     for name, *where in plan[1]:
         steps[name](*where)
 
+    def drain(ref, sem):
+        remote(ref, ref, sem, w_recv.at[0, q], far).wait_send()
+
     for piece in range(pieces):
-        for i in range(A):
-            ref = w_at(piece, q, x)
-            remote(
-                ref, ref, init_send.at[piece, i], w_recv.at[piece, q, x], far
-            ).wait_send()
-        for i in range(len(near_sources)):
-            far_relay(piece, i).wait_send()
-        for i in range(len(near_sources) + len(far_sources)):
-            pair_relay(piece, i).wait_send()
-    for k in range(chunks):
-        for copy in own_copies(k):
-            copy.wait_send()
-        pass_copy(k).wait_send()
-        for i in range(len(token_blocks)):
-            share_copy(i, k).wait_send()
-    for b in range(A):
-        kv_copy(0, g, b, quad[0]).wait_send()
-        kv_copy(1, g, b, far).wait_send()
-        kv_copy(2, 1 - g, b, quad[0]).wait_send()
+        drain(some_rows(piece, A), init_send.at[piece])
+        drain(some_rows(piece, near_count), far_send.at[piece])
+        drain(some_rows(piece, near_count + far_count), pair_send.at[piece])
+    half_rows = normed.at[0, pl.ds(0, half)]
+    for sem in (*(own_send.at[i] for i in range(3)), pass_send.at[0]):
+        drain(half_rows, sem)
+    for i in range(len(token_blocks)):
+        drain(half_rows, share_send.at[i])
+    for n in range(3):
+        drain(kvbuf.at[0, pl.ds(0, A)], kv_send.at[n])
     local_pick, sent_pick = pick_copies()
     local_pick.wait()
     sent_pick.wait()
     for h in range(hpg):
         own_out(h).wait()
-        for s in range(A - 1):
-            att_copy(h, s, order(s)).wait_send()
-        for t in (across, across_z, across_y):
-            cols = pl.ds(pl.multiple_of((t * hpg + h) * HD, HD), HD)
-            remote(
-                att.at[h, 0], out_ref.at[:, cols], att_send.at[h, 0], att_recv.at[h, t], sibling
-            ).wait_recv()
+        drain(att.at[h, pl.ds(0, A - 1)], att_send.at[h])
+    ref = kvbuf.at[0, pl.ds(0, hpg * (A - 1))]
+    remote(ref, ref, own_send.at[0], att_recv.at[0], sibling).wait_recv()
 
 
 def quad_plan(
@@ -1219,7 +1239,6 @@
     sizes = (A, rows, R, hpg, slots, blk, T, chunks, heads)
     pieces = hpg + 1
     dma = pltpu.SemaphoreType.DMA
-    smem = pl.BlockSpec(memory_space=pltpu.SMEM)
     anywhere = pl.BlockSpec(memory_space=pl.ANY)
     bf16, f32 = jnp.bfloat16, jnp.float32
     attended, cache = pl.pallas_call(
@@ -1228,9 +1247,13 @@
             pltpu.VMEM((rows, local_heads * HD), bf16),
             pltpu.VMEM((2 * count, HD), prev_kv.dtype),
         ),
-        in_specs=[smem] * 3 + [anywhere] * 7,
+        in_specs=[anywhere] * 10,
         out_specs=(anywhere, anywhere),
         scratch_shapes=[
+            pltpu.SMEM(block_order.shape, jnp.int32),
+            pltpu.SMEM(block_docs.shape, jnp.int32),
+            pltpu.SMEM(head_owner.shape, jnp.int32),
+            pltpu.VMEM((pieces, A, R // 2, HD), bf16),
             pltpu.VMEM((1, HD), f32),
             pltpu.VMEM((1, width), f32),
             pltpu.VMEM((rows // 2, width), bf16),
@@ -1245,19 +1268,22 @@
             pltpu.VMEM((kept * planes * heads, HD), bf16),
             pltpu.VMEM((2, count, HD), bf16),
             dma((pieces + 4,)),
-            dma((pieces, A)),
-            dma((pieces, A - 1)),
-            dma((pieces, n_seq - 1)),
-            dma((pieces, n_seq, 2)),
+            dma((pieces,)),
+            dma((3,)),
+            dma((pieces,)),
+            dma((pieces,)),
+            dma((pieces,)),
+            dma((pieces, n_seq)),
+            dma((pieces, 2)),
+            dma((3,)),
+            dma((1,)),
+            dma((3,)),
             dma((3, chunks)),
-            dma((chunks,)),
-            dma((3, chunks)),
-            dma((3, chunks)),
-            dma((4, chunks)),
-            dma((3, A)),
-            dma((3, A)),
-            dma((hpg, A)),
-            dma((hpg, A)),
+            dma((1,)),
+            dma((3,)),
+            dma((A + 2,)),
+            dma((hpg,)),
+            dma((1,)),
             dma((hpg,)),
             dma((3,)),
         ],

time: 66.7 us -> 63.1 us (0.946)
  Pallas kernels: 64.5 us -> 61 us
    pallas_call x1, Pallas kernels: 64.5 us -> 61 us  [quad_plan(): pl.pallas_call(functools.partial(quad_kernel, (first_own, PLAN), sizes),...]
where the time goes in v3:
time: 63.1 us; the launch traced here: 63 us
  Pallas kernels  61 us (97%)
  local copies, waits for them, and re-layouts  1.36 us (2%)
  between operations  0.64 us (1%)
    pallas_call x1, Pallas kernels, quad_plan(): pl.pallas_call(functools.partial(quad_kernel, (first_own, PLAN), sizes),...  61 us
    unnamed x2, local copies, waits for them, and re-layouts  1.36 us

profile of v3, /device:TPU:0, one launch (start us, length us, event | category | flops | bytes accessed | tf_op | source)
XLA Modules:
  0.0 63.0 jit_solution(11838156671260042621)
XLA Ops:
  0.6 61.0 %shard_map.113 = (bf16[128,1024]{1,0:T(8,128)(2,1)S(1)}, bf16[512,128]{1,0:T(8,128)(2,1)S(1)}) custom-call(s32[16]{0:T(128)} %order_in.1, s32[16]{0:T(128)} %docs_in.1, s32[4]{0:T(128)} %owner_in.1, f32[1,128]{1,0:T(1,128)} %constant.2.clone.freq_in, f32[1,4096]{1,0:T(1,128)} %bitcast.5, bf16[128,4096]{1,0:T(8,128)(2,1)} %tok_in.1, bf16[512,1024]{1,0:T(8,128)(2,1)} %wq_in.1, ...), custom_call_target="tpu_custom_call" | custom-call | tf_op jit(solution)/shard_map/pallas_call | solution.py:1244
  61.6 0.7 %copy.14 = bf16[128,1024]{1,0:T(8,128)(2,1)} copy(bf16[128,1024]{1,0:T(8,128)(2,1)S(1)} %get-tuple-element.6) | data formatting | bytes 524288
  62.3 0.7 %copy.15 = bf16[128,2,2,128]{3,2,1,0:T(2,128)(2,1)} copy(bf16[128,2,2,128]{3,2,1,0:T(2,128)(2,1)S(1)} %bitcast.3) | data formatting | bytes 262144

commit v4 on v3

--- a/solution.py
+++ b/solution.py
@@ -666,17 +666,17 @@
 
 
 PLAN = (
-    ("first", 0, 2), ("first", 1, 1), ("spare", 1), ("first", 0, 1), ("first", 1, 0),
-    ("first", 2, 3), ("first", 0, 3), ("first", 1, 2), ("own", 2), ("near", 2, 0), ("own", 1),
-    ("first", 0, 0), ("near", 0, 2), ("own", 0), ("near", 0, 1), ("tok", 0, 2), ("tok", 1, 2),
-    ("near", 1, 2), ("own", 3), ("far", 0, 3), ("tok", 2, 2), ("first", 1, 3), ("near", 0, 0),
-    ("tok", 1, 1), ("tok", 0, 1), ("near", 1, 1), ("tok", 0, 0), ("far", 0, 0), ("spare", 0),
-    ("tok", 1, 0), ("first", 2, 0), ("near", 1, 0), ("first", 2, 2), ("far", 2, 1),
-    ("far", 0, 2), ("far", 1, 0), ("tok", 0, 3), ("tok", 1, 3), ("far", 0, 1), ("near", 2, 1),
-    ("tok", 2, 3), ("tok", 2, 1), ("far", 1, 3), ("tok", 2, 0), ("first", 2, 1),
-    ("far", 1, 1), ("far", 1, 2), ("keys",), ("far", 2, 2), ("near", 2, 2), ("kv", 1),
-    ("kv", 0), ("far", 2, 0), ("query",), ("far", 2, 3), ("early",), ("kv", 2), ("head",),
-    ("last",),
+    ("first", 2, 3), ("first", 1, 3), ("first", 0, 1), ("first", 0, 2), ("first", 0, 0),
+    ("own", 1), ("first", 0, 3), ("near", 0, 1), ("far", 0, 0), ("own", 2), ("near", 1, 0),
+    ("own", 0), ("tok", 0, 2), ("near", 0, 2), ("near", 0, 0), ("first", 1, 2),
+    ("first", 1, 1), ("first", 1, 0), ("tok", 1, 2), ("own", 3), ("first", 2, 1),
+    ("tok", 0, 0), ("far", 0, 3), ("tok", 0, 1), ("near", 2, 0), ("spare", 1), ("near", 1, 1),
+    ("first", 2, 0), ("far", 0, 2), ("far", 0, 1), ("far", 1, 0), ("near", 1, 2),
+    ("tok", 0, 3), ("first", 2, 2), ("far", 2, 1), ("tok", 2, 3), ("near", 2, 2),
+    ("tok", 2, 1), ("tok", 2, 0), ("spare", 0), ("tok", 1, 3), ("tok", 2, 2), ("tok", 1, 1),
+    ("tok", 1, 0), ("far", 1, 2), ("far", 1, 1), ("keys",), ("near", 2, 1), ("early", 1, 0),
+    ("far", 1, 3), ("far", 2, 0), ("early", 2, 0), ("early", 1, 1), ("far", 2, 3), ("kv", 1),
+    ("query",), ("far", 2, 2), ("early", 2, 1), ("kv", 0), ("kv", 2), ("head",), ("last",),
 )
 
 
@@ -767,6 +767,11 @@
     far = dev(x, (1 - g) * A + c, d)
     quad = [dev(x, g * A + t, d) for t in (across_y, across_z, across)]
 
+    barrier = pltpu.get_barrier_semaphore()
+    peers = quad + [far, pair, sibling]
+    for peer in peers:
+        pl.semaphore_signal(barrier, inc=1, device_id=peer, device_id_type=pl.DeviceIdType.MESH)
+
     def w_at(piece, source, part):
         return wbuf.at[piece, pl.ds(pl.multiple_of(source * R + part * Rp, Rp), Rp)]
 
@@ -822,10 +827,6 @@
     for copy in table_copies:
         copy.start()
 
-    barrier = pltpu.get_barrier_semaphore()
-    peers = quad + [far, pair, sibling]
-    for peer in peers:
-        pl.semaphore_signal(barrier, inc=1, device_id=peer, device_id_type=pl.DeviceIdType.MESH)
     pl.semaphore_wait(barrier, len(peers))
 
     targets = ((c, far), (across, quad[2]), (across_z, quad[1]), (across_y, quad[0]))
@@ -1069,7 +1070,7 @@
         back = A - 1 - s
         return near(back // 2, back % 2)
 
-    def attend(h, pair_id, blocks, queries):
+    def attend(h, blocks, queries, push=True):
         scores = lax.dot_general(
             jnp.concatenate(queries, 0),
             kvbuf[0].reshape(T, HD),
@@ -1086,19 +1087,15 @@
         done = (weighted / total).astype(jnp.bfloat16)
         for i, b in enumerate(blocks):
             att[h, b] = done[i * rows : (i + 1) * rows]
-        att_copy(h, blocks[0]).start()
-
-        @pl.when(pair_id < A // 2 - 1)
-        def _():
-            att_copy(h, blocks[1]).start()
+        if push:
+            for b in blocks:
+                att_copy(h, b).start()
 
     def attend_all(h, query):
-        def attend_pair(s, carry):
-            blocks = [order(2 * s), order(2 * s + 1)]
-            attend(h, s, blocks, [query(b) for b in blocks])
-            return carry
-
-        lax.fori_loop(0, A // 2, attend_pair, 0)
+        blocks = [across, across_z]
+        attend(h, blocks, [query(b) for b in blocks])
+        attend(h, [across_y], [query(across_y)])
+        attend(h, [c], [query(c)], False)
         own_out(h).start()
 
     def own_tokens(k):
@@ -1131,11 +1128,12 @@
         lax.fori_loop(0, A, project_kv, 0)
 
     def project_first():
-        arrive_pair(1, 0, len(near_sources) + len(far_sources))
+        arrive_pair(1, 0, near_count + far_count)
+        late = [span_of(source, 1 - x) for source in near_sources + far_sources]
 
         def project(s, carry):
             b = order(s)
-            product = jnp.dot(normed[b], wbuf[1], preferred_element_type=jnp.float32)
+            product = acc[0, b] + partial(1, b, late)
             qbuf[b] = turn(product, b).astype(jnp.bfloat16)
             return carry
 
@@ -1147,12 +1145,16 @@
     last = hpg
     near_count, far_count = len(near_sources), len(far_sources)
 
-    def project_early():
-        early = [span_of(q, 0), span_of(q, 1)]
-        early += [span_of(source, x) for source in near_sources]
+    def project_early(piece, group):
+        if group:
+            spans = [span_of(source, x) for source in far_sources]
+        else:
+            spans = [span_of(q, 0), span_of(q, 1)]
+            spans += [span_of(source, x) for source in near_sources]
 
         def project(b, carry):
-            acc[b] = partial(last, b, early)
+            term = partial(piece, b, spans)
+            acc[piece - 1, b] = acc[piece - 1, b] + term if group else term
             return carry
 
         lax.fori_loop(0, A, project, 0)
@@ -1160,10 +1162,9 @@
     def attend_last():
         arrive_pair(last, 0, near_count)
         middle = [span_of(source, 1 - x) for source in near_sources]
-        middle += [span_of(source, x) for source in far_sources]
 
         def project(b, carry):
-            acc[b] += partial(last, b, middle)
+            acc[last - 1, b] += partial(last, b, middle)
             return carry
 
         lax.fori_loop(0, A, project, 0)
@@ -1171,7 +1172,7 @@
         late = [span_of(source, 1 - x) for source in far_sources]
 
         def query(b):
-            return turn(acc[b] + partial(last, b, late), b).astype(jnp.bfloat16)
+            return turn(acc[last - 1, b] + partial(last, b, late), b).astype(jnp.bfloat16)
 
         attend_all(1, query)
 
@@ -1260,7 +1261,7 @@
             pltpu.VMEM((pieces, width, HD), bf16),
             pltpu.VMEM((A, rows, width), bf16),
             pltpu.VMEM((A, rows, HD), bf16),
-            pltpu.VMEM((A, rows, HD), f32),
+            pltpu.VMEM((hpg, A, rows, HD), f32),
             pltpu.VMEM((2, n_seq, rows, HD), bf16),
             pltpu.VMEM((2, A, rows, HD), f32),
             pltpu.VMEM((A, rows, T), f32),

time: 63.1 us -> 62.5 us (level)
  Pallas kernels: 61 us -> 60.3 us
    pallas_call x1, Pallas kernels: 61 us -> 60.3 us  [quad_plan(): pl.pallas_call(functools.partial(quad_kernel, (first_own, PLAN), sizes),...]
where the time goes in v4:
time: 62.5 us; the launch traced here: 62.3 us
  Pallas kernels  60.3 us (96%)
  local copies, waits for them, and re-layouts  1.36 us (2%)
  between operations  0.64 us (1%)
    pallas_call x1, Pallas kernels, quad_plan(): pl.pallas_call(functools.partial(quad_kernel, (first_own, PLAN), sizes),...  60.3 us
    unnamed x2, local copies, waits for them, and re-layouts  1.36 us

profile of v4, /device:TPU:0, one launch (start us, length us, event | category | flops | bytes accessed | tf_op | source)
XLA Modules:
  0.0 62.3 jit_solution(6072135751916471166)
XLA Ops:
  0.6 60.3 %shard_map.113 = (bf16[128,1024]{1,0:T(8,128)(2,1)S(1)}, bf16[512,128]{1,0:T(8,128)(2,1)S(1)}) custom-call(s32[16]{0:T(128)} %order_in.1, s32[16]{0:T(128)} %docs_in.1, s32[4]{0:T(128)} %owner_in.1, f32[1,128]{1,0:T(1,128)} %constant.2.clone.freq_in, f32[1,4096]{1,0:T(1,128)} %bitcast.5, bf16[128,4096]{1,0:T(8,128)(2,1)} %tok_in.1, bf16[512,1024]{1,0:T(8,128)(2,1)} %wq_in.1, ...), custom_call_target="tpu_custom_call" | custom-call | tf_op jit(solution)/shard_map/pallas_call | solution.py:1245
  60.9 0.7 %copy.14 = bf16[128,1024]{1,0:T(8,128)(2,1)} copy(bf16[128,1024]{1,0:T(8,128)(2,1)S(1)} %get-tuple-element.6) | data formatting | bytes 524288
  61.6 0.7 %copy.15 = bf16[128,2,2,128]{3,2,1,0:T(2,128)(2,1)} copy(bf16[128,2,2,128]{3,2,1,0:T(2,128)(2,1)S(1)} %bitcast.3) | data formatting | bytes 262144
